TPU v7x, 128 devices: a whole 4x4x4 slice. The times are simulated.
128 devices in a mesh: dp: 2 (over core), seq: 16 (over y, x), tensor: 4 (over z).
Axes of the slice: x: 4, y: 4, z: 4, core: 2. Of those that a mesh axis runs over, the one named last changes fastest.
Arguments:
- tokens: bfloat16 [2, 8192, 2048], P('dp', ('seq', 'tensor')), may hold values from -6 to 6
- attn_gain: float32 [2048], replicated, may hold values from 0.5 to 1.5
- w_qkv: bfloat16 [3, 2048, 2048], P(None, None, 'tensor'), may hold values from -1 to 1
- w_out: bfloat16 [2048, 2048], P('tensor'), may hold values from -0.125 to 0.125
- mlp_gain: float32 [2048], replicated, may hold values from 0.5 to 1.5
- w_up: bfloat16 [2048, 8192], P(None, 'tensor'), may hold values from -0.125 to 0.125
- w_down: bfloat16 [8192, 2048], P('tensor'), may hold values from -0.0625 to 0.0625
- pool_gain: float32 [2048], replicated, may hold values from -8 to 8
- pool_bias: float32 [2048], replicated, may hold values from 0.5 to 5
- value_weight: float32 [2048], replicated, may hold values from -6 to 6
- valid_frames: int32 [2], replicated, may hold values from 16 to 32, as said below
Outputs:
- hidden: bfloat16 [2, 8192, 2048], P('dp', ('seq', 'tensor'))
- frame_values: float32 [2, 32], P('dp', 'seq')
- advantages: float32 [2, 32], P('dp', 'seq')
Inputs may be any that keep to these rules, and one draw needn't show every extreme that they name: `valid_frames`: at least one rollout keeps all 32 frames and at least one keeps 32 // 2 of them.
All inputs are finite; a program needn't handle non-finite values.
Results may differ from a plain program's by a relative error of at most 0.017.
Values may be sent and summed in bfloat16 or wider, within the bound.
A program may use at most 256 MiB of HBM per device.

v0:
```python
import jax
import jax.numpy as jnp
from jax import lax
from jax.sharding import PartitionSpec as P

HEAD_DIM = 128
TOK_FRAME = 256
FR_DEV = 2


def laid_out(blocks, dim):
    shape = list(blocks.shape[1:])
    shape[dim] *= blocks.shape[0]
    return jnp.moveaxis(blocks, 0, dim).reshape(shape)


def sent_to_all(array, axis):
    copies = jnp.broadcast_to(array, (lax.axis_size(axis), *array.shape))
    return lax.all_to_all(copies, axis, split_axis=0, concat_axis=0, tiled=True)


def gathered_copies(array, axis, dim):
    return laid_out(sent_to_all(array, axis), dim)


def cut_along(array, dim, size):
    shape = array.shape
    blocks = array.reshape(*shape[:dim], size, shape[dim] // size, *shape[dim + 1 :])
    return jnp.moveaxis(blocks, dim, 0)


def summed_on_arrival(array, axis, dim):
    size = lax.axis_size(axis)
    blocks = lax.all_to_all(cut_along(array, dim, size), axis, 0, 0, tiled=True)
    return jnp.sum(blocks.astype(jnp.float32), axis=0)


def over_copies(array, axis):
    everything = sent_to_all(array, axis)
    return jnp.sum(everything, axis=0)


def collected_together(array, axis):
    leaves = jax.tree.leaves(array)
    sequence = sorted(range(len(leaves)), key=lambda k: -leaves[k].size)
    width = (1, *leaves[sequence[0]].shape)[-1]
    lines = [
        jnp.pad(leaves[k].reshape(-1), (0, -leaves[k].size % width)).reshape(-1, width)
        for k in sequence
    ]
    both, at, found = (sent_to_all(jnp.concatenate(lines), axis), 0, {})
    for k, line in zip(sequence, lines):
        piece = both[:, at : at + len(line)].reshape(len(both), -1)
        found[k] = piece[:, : leaves[k].size].reshape(-1, *leaves[k].shape)
        at += len(line)
    numbers = iter(range(len(leaves)))
    return jax.tree.map(lambda _: found[next(numbers)], array)


def combined_pairwise(pieces, combine):
    while len(jax.tree.leaves(pieces)[0]) > 1:
        pieces = jax.vmap(combine)(
            *(jax.tree.map(lambda part: part[side::2], pieces) for side in (0, 1))
        )
    return jax.tree.map(lambda part: part[0], pieces)


def entering_2(array, axis, combine, identity):
    size, index = (lax.axis_size(axis), lax.axis_index(axis))
    passed = jnp.arange(size) < index

    def kept(part, zero, own):
        part = jnp.where(
            passed.reshape(-1, *(1 for _ in own.shape)), part, jnp.asarray(zero, own.dtype)
        )
        return part

    pieces = collected_together(array, axis)
    return combined_pairwise(jax.tree.map(kept, pieces, identity, array), combine)


def rms_norm(values, gain):
    floats = values.astype(jnp.float32)
    square = jnp.mean(floats * floats, axis=-1, keepdims=True)
    return (floats * lax.rsqrt(square + 1e-05) * gain).astype(jnp.bfloat16)


def compose(earlier, later):
    return (earlier[0] * later[0], later[0] * earlier[1] + later[1])


def local(
    tokens,
    attn_gain,
    w_qkv,
    w_out,
    mlp_gain,
    w_up,
    w_down,
    pool_gain,
    pool_bias,
    value_weight,
    valid_frames,
):
    rows = tokens[0]
    row_count = rows.shape[0]
    seq_index = lax.axis_index("seq")
    tensor_index = lax.axis_index("tensor")
    roll_index = lax.axis_index("dp")
    length = valid_frames[roll_index]
    local_heads = w_qkv.shape[2] // HEAD_DIM
    scale = 1.0 / HEAD_DIM**0.5
    normed = rms_norm(rows, attn_gain)
    qkv = jnp.einsum(
        "nd,cde->nce",
        gathered_copies(normed, "tensor", 0),
        w_qkv,
        preferred_element_type=jnp.float32,
    ).astype(jnp.bfloat16)
    block = qkv.shape[0]
    query = qkv[:, 0].reshape(block, local_heads, HEAD_DIM)
    query_frame = (seq_index * block + jnp.arange(block, dtype=jnp.int32)) // TOK_FRAME
    peak = jnp.full((local_heads, block), -1e30, jnp.float32)
    key_piece = lax.all_gather(qkv[:, 1], "seq", axis=0, tiled=True)
    value_piece = lax.all_gather(qkv[:, 2], "seq", axis=0, tiled=True)
    width = key_piece.shape[0]
    key_heads = key_piece.reshape(width, local_heads, HEAD_DIM)
    value_heads = value_piece.reshape(width, local_heads, HEAD_DIM)
    scores = (
        jnp.einsum("qhe,khe->hqk", query, key_heads, preferred_element_type=jnp.float32) * scale
    )
    key_frame = jnp.arange(width, dtype=jnp.int32) // TOK_FRAME
    allowed = (key_frame[None, :] <= query_frame[:, None]) & (key_frame[None, :] < length)
    scores = jnp.where(allowed[None], scores, -1e30)
    new_peak = jnp.maximum(peak, jnp.max(scores, axis=-1))
    weights = jnp.where(allowed[None], jnp.exp(scores - new_peak[..., None]), 0.0)
    total = jnp.sum(weights, axis=-1)
    acc = jnp.einsum(
        "hqk,khe->hqe",
        weights.astype(jnp.bfloat16),
        value_heads,
        preferred_element_type=jnp.float32,
    )
    peak, total, acc = (new_peak, total, acc)
    mixed = (
        (acc / total[..., None])
        .transpose(1, 0, 2)
        .reshape(block, local_heads * HEAD_DIM)
        .astype(jnp.bfloat16)
    )
    attn_sum = summed_on_arrival(
        jnp.dot(mixed, w_out, preferred_element_type=jnp.float32).astype(jnp.bfloat16), "tensor", 0
    )
    after_attn = (rows.astype(jnp.float32) + attn_sum).astype(jnp.bfloat16)
    normed2 = rms_norm(after_attn, mlp_gain)
    up = jax.nn.gelu(
        jnp.dot(gathered_copies(normed2, "tensor", 0), w_up, preferred_element_type=jnp.float32),
        approximate=True,
    ).astype(jnp.bfloat16)
    down_sum = summed_on_arrival(
        jnp.dot(up, w_down, preferred_element_type=jnp.float32).astype(jnp.bfloat16), "tensor", 0
    )
    hidden = (after_attn.astype(jnp.float32) + down_sum).astype(jnp.bfloat16)
    local_frame = (tensor_index * row_count + jnp.arange(row_count, dtype=jnp.int32)) // TOK_FRAME
    selector = (local_frame[None, :] == jnp.arange(FR_DEV, dtype=jnp.int32)[:, None]).astype(
        jnp.bfloat16
    )
    sums = jnp.dot(selector, hidden, preferred_element_type=jnp.float32)
    sums = over_copies(sums, "tensor")
    gain, offset, head_weight = (pool_gain, pool_bias, value_weight)
    means = sums / TOK_FRAME
    frame_global = seq_index * FR_DEV + jnp.arange(FR_DEV, dtype=jnp.int32)
    valid = frame_global < length
    gate = jax.nn.sigmoid(means * gain + offset)
    decay = jnp.where(valid[:, None], gate, 1.0)
    source = jnp.where(valid[:, None], (1.0 - gate) * means, 0.0)
    agg_decay = jnp.ones_like(means[0])
    agg_source = jnp.zeros_like(means[0])
    for frame in range(FR_DEV):
        agg_decay, agg_source = compose((agg_decay, agg_source), (decay[frame], source[frame]))
    entering = entering_2(
        (agg_decay, agg_source),
        "seq",
        compose,
        (jnp.ones_like(agg_decay), jnp.zeros_like(agg_source)),
    )
    state = entering[1]
    collected = []
    for frame in range(FR_DEV):
        state = decay[frame] * state + source[frame]
        collected.append(jnp.sum(state * head_weight))
    partial_values = jnp.stack(collected)
    values = jnp.where(valid, partial_values, 0.0)
    pick = jnp.sum(jnp.where(frame_global == length - 1, values, 0.0))
    count = jnp.sum(valid_frames).astype(jnp.float32)
    slot = (jnp.arange(lax.axis_size("dp"), dtype=jnp.int32) == roll_index).astype(jnp.float32)
    entries = jnp.stack([pick, jnp.sum(values), jnp.sum(values * values)])
    table = over_copies(entries[:, None] * slot[None, :], ("dp", "seq"))
    finals, first_sums, second_sums = (table[0], table[1], table[2])
    lengths = valid_frames.astype(jnp.float32)
    mean = jnp.sum(lengths * finals - first_sums) / count
    squares = jnp.sum(lengths * finals * finals - 2.0 * finals * first_sums + second_sums) / count
    variance = squares - mean * mean
    final = jnp.sum(finals * slot)
    gap = jnp.where(valid, final - values, 0.0)
    centered = jnp.where(valid, gap - mean, 0.0)
    advantages = jnp.where(valid, centered * lax.rsqrt(variance + 1e-05), 0.0)
    return (hidden[None], values[None], advantages[None])


def solution(mesh):
    in_specs = (
        P("dp", ("seq", "tensor"), None),
        P(),
        P(None, None, "tensor"),
        P("tensor", None),
        P(),
        P(None, "tensor"),
        P("tensor", None),
        P(),
        P(),
        P(),
        P(),
    )
    out_specs = (P("dp", ("seq", "tensor"), None), P("dp", "seq"), P("dp", "seq"))
    return jax.shard_map(local, mesh=mesh, in_specs=in_specs, out_specs=out_specs, check_vma=False)
```

profile of v0, /device:TPU:1, one launch (start us, length us, event | category | flops | bytes accessed | tf_op | source)
XLA Modules:
  0.0 397.9 jit_solution(1395034552048912833)
XLA Ops:
  10.6 31.1 %all_to_all.35 = bf16[4,128,2048]{2,1,0:T(8,128)(2,1)S(1)} all-to-all(bf16[4,128,2048]{2,1,0:T(8,128)(2,1)S(1)} %broadcast_in_dim.104), channel_id=1, replica_groups=mesh['dp'=2,'seq'=16,'tensor'=4] {'tensor'}, dimensions={0} | all-to-all | bytes 4194304 | tf_op jit(solution)/shard_map/all_to_all | solution.py:19
  41.7 3.5 convolution_convert_fusion.2
  48.3 4.9 %compare_and_fusion = pred[512,8192]{1,0:T(8,128)(4,1)} fusion(s32[8192]{0:T(1024)S(1)} %add_select_fusion, s32[512]{0:T(512)S(1)} %add_select_fusion.1, pred[8192]{0:T(1024)(128)(4,1)S(1)} %broadcast_compare_fusion), kind=kLoop, calls=%fused_computation.7 | loop fusion | flops 8388608 | bytes 4237312 | tf_op jit(solution)/shard_map/and | solution.py:133
  53.2 69.6 %all-gather.5.cloned.1.call-done = bf16[8192,1,512]{0,2,1:T(8,128)(2,1)} async-done(((bf16[512,1,512]{0,2,1:T(8,128)(2,1)}), bf16[8192,1,512]{0,2,1:T(8,128)(2,1)}) %all-gather.5.cloned.1.call-update) | async-done | bytes 8388624 | tf_op jit(solution)/shard_map/all_gather | solution.py:124
  122.8 30.0 %fusion = (f32[4,512]{1,0:T(4,128)S(1)}, f32[4,512,8192]{2,1,0:T(8,128)}) fusion(pred[512,8192]{1,0:T(8,128)(4,1)} %compare_and_fusion, bf16[512,4,128]{0,2,1:T(8,128)(2,1)S(1)} %bitcast.73, bf16[8192,4,128]{0,2,1:T(8,128)(2,1)} %bitcast.78), kind=kOutput, calls=%fused_computation.2 | convolution fusion | flops 4345296896 | bytes 80224256 | tf_op jit(solution)/shard_map/qhe,khe->hqk/dot_general | solution.py:130
  152.8 23.6 %fusion.1 = f32[4,512]{1,0:T(4,128)S(1)} fusion(f32[4,512,8192]{2,1,0:T(8,128)} %get-tuple-element.36, f32[4,512]{1,0:T(4,128)S(1)} %broadcast_maximum_fusion, pred[512,8192]{1,0:T(8,128)(4,1)} %compare_and_fusion), kind=kLoop, calls=%fused_computation.3 | loop fusion | flops 83884032 | bytes 71319552 | tf_op jit(solution)/shard_map/reduce_sum | solution.py:137
  176.4 25.0 %all-gather.7.cloned.1.call-done = bf16[8192,1,512]{0,2,1:T(8,128)(2,1)} async-done(((bf16[512,1,512]{0,2,1:T(8,128)(2,1)}), bf16[8192,1,512]{0,2,1:T(8,128)(2,1)}) %all-gather.7.cloned.1.call-update) | async-done | bytes 8388624 | tf_op jit(solution)/shard_map/all_gather | solution.py:125
  201.4 28.9 %divide_convert_fusion = bf16[512,4,128]{0,2,1:T(8,128)(2,1)S(1)} fusion(bf16[8192,4,128]{0,2,1:T(8,128)(2,1)} %bitcast.79, f32[4,512,8192]{2,1,0:T(8,128)} %get-tuple-element.36, f32[4,512]{1,0:T(4,128)S(1)} %broadcast_maximum_fusion, pred[512,8192]{1,0:T(8,128)(4,1)} %compare_and_fusion, f32[512,4]{0,1:T(4,128)S(1)} %bitcast.77), kind=kOutput, calls=%fused_computation.46 | convolution fusion | flops 4379377664 | bytes 80232448 | tf_op jit(solution)/shard_map/hqk,khe->hqe/dot_general | solution.py:138
  231.7 28.0 %all_to_all.36 = bf16[4,128,2048]{2,1,0:T(8,128)(2,1)S(1)} all-to-all(bf16[4,128,2048]{2,1,0:T(8,128)(2,1)S(1)} %bitcast.71), channel_id=1, replica_groups=mesh['dp'=2,'seq'=16,'tensor'=4] {'tensor'}, dimensions={0} | all-to-all | bytes 4194304 | tf_op jit(solution)/shard_map/all_to_all | solution.py:34
  261.6 26.4 %all_to_all.37 = bf16[4,128,2048]{2,1,0:T(8,128)(2,1)} all-to-all(bf16[4,128,2048]{2,1,0:T(8,128)(2,1)S(1)} %broadcast_in_dim.108), channel_id=1, replica_groups=mesh['dp'=2,'seq'=16,'tensor'=4] {'tensor'}, dimensions={0} | all-to-all | bytes 4194304 | tf_op jit(solution)/shard_map/all_to_all | solution.py:19
  288.0 16.6 %convolution_convert_fusion = bf16[512,2048]{1,0:T(8,128)(2,1)} fusion(bf16[2048,2048]{1,0:T(8,128)(2,1)} %param.17, bf16[512,2048]{1,0:T(8,128)(2,1)} %bitcast.72, bf16[2048,2048]{1,0:T(8,128)(2,1)} %param.16), kind=kOutput, calls=%fused_computation.19 | convolution fusion | flops 8600420352 | bytes 20971520 | tf_op jit(solution)/shard_map/dot_general | solution.py:161
  304.6 4.6 %all-to-all-start.3 = ((bf16[4,128,2048]{2,1,0:T(8,128)(2,1)}), bf16[4,128,2048]{2,1,0:T(8,128)(2,1)}, u32[]{:S(2)}, u32[]{:S(2)}) async-start(bf16[4,128,2048]{2,1,0:T(8,128)(2,1)} %bitcast.69), calls=%async_computation.3 | async-start | bytes 4194304 | tf_op jit(solution)/shard_map/all_to_all | solution.py:34
  309.2 22.3 %all-to-all-done.3 = bf16[4,128,2048]{2,1,0:T(8,128)(2,1)} async-done(((bf16[4,128,2048]{2,1,0:T(8,128)(2,1)}), bf16[4,128,2048]{2,1,0:T(8,128)(2,1)}, u32[]{:S(2)}, u32[]{:S(2)}) %all-to-all-start.3) | async-done | bytes 2097184 | tf_op jit(solution)/shard_map/all_to_all | solution.py:34
  331.5 2.1 convert_reduce_fusion
  336.6 3.3 all-to-all-start.4
  340.5 3.8 all-to-all-done.4
  345.9 4.7 %all-to-all-start.5 = ((f32[16,2,2048]{2,1,0:T(2,128)}), f32[16,2,2048]{2,1,0:T(2,128)S(1)}, u32[]{:S(2)}, u32[]{:S(2)}) async-start(f32[16,2,2048]{2,1,0:T(2,128)} %broadcast_in_dim.113), calls=%async_computation.5 | async-start | bytes 524288 | tf_op jit(solution)/shard_map/all_to_all | solution.py:19
  353.1 5.0 %all-to-all-done.5 = f32[16,2,2048]{2,1,0:T(2,128)S(1)} async-done(((f32[16,2,2048]{2,1,0:T(2,128)}), f32[16,2,2048]{2,1,0:T(2,128)S(1)}, u32[]{:S(2)}, u32[]{:S(2)}) %all-to-all-start.5) | async-done | bytes 262176 | tf_op jit(solution)/shard_map/all_to_all | solution.py:19
  361.1 2.5 fusion.52
  363.6 2.0 pad_maximum_fusion.1
  366.9 11.1 %all-to-all-start.6 = ((f32[32,3,2]{1,2,0:T(2,128)}), f32[32,3,2]{1,2,0:T(2,128)S(1)}, u32[]{:S(2)}, u32[]{:S(2)}) async-start(f32[32,3,2]{1,2,0:T(2,128)} %broadcast_in_dim.118), calls=%async_computation.6 | async-start | bytes 65536 | tf_op jit(solution)/shard_map/all_to_all | solution.py:19
  378.1 2.3 fusion.34
  380.4 4.7 %all-to-all-done.6 = f32[32,3,2]{1,2,0:T(2,128)S(1)} async-done(((f32[32,3,2]{1,2,0:T(2,128)}), f32[32,3,2]{1,2,0:T(2,128)S(1)}, u32[]{:S(2)}, u32[]{:S(2)}) %all-to-all-start.6) | async-done | bytes 800 | tf_op jit(solution)/shard_map/all_to_all | solution.py:19
  388.0 3.1 multiply_select_fusion.2
  (78 shorter events, 21.8 us)
Async XLA Ops:
  7.2 223.2 %copy-start = (bf16[512,2048]{1,0:T(8,128)(2,1)S(1)}, bf16[512,2048]{1,0:T(8,128)(2,1)}, u32[]{:S(2)}) copy-start(bf16[512,2048]{1,0:T(8,128)(2,1)} %param.14) | copy-start | bytes 6291460
  7.2 115.6 %all-gather.5.cloned.1.call-start = ((), (), s32[]{:S(2)}) async-start(), calls=%async_computation.7 | async-start | bytes 8912896 | tf_op jit(solution)/shard_map/all_gather | solution.py:124
  7.2 34.5 %copy-start.9 = (bf16[3,2048,512]{2,1,0:T(8,128)(2,1)S(1)}, bf16[3,2048,512]{2,1,0:T(8,128)(2,1)}, u32[]{:S(2)}) copy-start(bf16[3,2048,512]{2,1,0:T(8,128)(2,1)} %param.13) | copy-start | bytes 18874372
  41.7 5.3 %copy-start.8 = (s32[2]{0:T(128)S(1)}, s32[2]{0:T(128)}, u32[]{:S(2)}) copy-start(s32[2]{0:T(128)} %param.21) | copy-start | bytes 28
  46.3 155.1 %all-gather.7.cloned.1.call-start = ((), (), s32[]{:S(2)}) async-start(), calls=%async_computation.8 | async-start | bytes 8912896 | tf_op jit(solution)/shard_map/all_gather | solution.py:125
  230.4 29.7 %copy-start.2 = (bf16[1,128,2048]{2,1,0:T(8,128)(2,1)S(1)}, bf16[1,128,2048]{2,1,0:T(8,128)(2,1)}, u32[]{:S(2)}) copy-start(bf16[1,128,2048]{2,1,0:T(8,128)(2,1)} %param.11) | copy-start | bytes 1572868
  230.4 30.7 %copy-start.5 = (f32[2048]{0:T(1024)S(1)}, f32[2048]{0:T(1024)}, u32[]{:S(2)}) copy-start(f32[2048]{0:T(1024)} %param.15) | copy-start | bytes 24580
  260.3 0.8 copy-start.3
  288.0 21.2 %copy-start.6 = (f32[2048]{0:T(1024)S(1)}, f32[2048]{0:T(1024)}, u32[]{:S(2)}) copy-start(f32[2048]{0:T(1024)} %param.18) | copy-start | bytes 24580
  304.6 39.8 %copy-start.7 = (f32[2048]{0:T(1024)S(1)}, f32[2048]{0:T(1024)}, u32[]{:S(2)}) copy-start(f32[2048]{0:T(1024)} %param.19) | copy-start | bytes 24580
  304.6 27.0 %all-to-all-start.3 = ((bf16[4,128,2048]{2,1,0:T(8,128)(2,1)}), bf16[4,128,2048]{2,1,0:T(8,128)(2,1)}, u32[]{:S(2)}, u32[]{:S(2)}) async-start(bf16[4,128,2048]{2,1,0:T(8,128)(2,1)} %bitcast.69), calls=%async_computation.3 | async-start | bytes 4194304 | tf_op jit(solution)/shard_map/all_to_all | solution.py:34
  333.7 1.0 copy-start.1
  336.6 7.7 %all-to-all-start.4 = ((f32[4,2,2048]{2,1,0:T(2,128)}), f32[4,2,2048]{2,1,0:T(2,128)S(1)}, u32[]{:S(2)}, u32[]{:S(2)}) async-start(f32[4,2,2048]{2,1,0:T(2,128)} %broadcast_in_dim.110), calls=%async_computation.4 | async-start | bytes 131072 | tf_op jit(solution)/shard_map/all_to_all | solution.py:19
  344.4 1.5 copy-start.4
  345.9 12.2 %all-to-all-start.5 = ((f32[16,2,2048]{2,1,0:T(2,128)}), f32[16,2,2048]{2,1,0:T(2,128)S(1)}, u32[]{:S(2)}, u32[]{:S(2)}) async-start(f32[16,2,2048]{2,1,0:T(2,128)} %broadcast_in_dim.113), calls=%async_computation.5 | async-start | bytes 524288 | tf_op jit(solution)/shard_map/all_to_all | solution.py:19
  366.9 18.1 %all-to-all-start.6 = ((f32[32,3,2]{1,2,0:T(2,128)}), f32[32,3,2]{1,2,0:T(2,128)S(1)}, u32[]{:S(2)}, u32[]{:S(2)}) async-start(f32[32,3,2]{1,2,0:T(2,128)} %broadcast_in_dim.118), calls=%async_computation.6 | async-start | bytes 65536 | tf_op jit(solution)/shard_map/all_to_all | solution.py:19
Sparse Core Ops, SparseCore 0:
  46.4 76.3 all-gather.4
  124.9 76.4 all-gather.6
where the time goes:
time: 399 us; the launch traced here: 398 us
  waiting for transfers between devices  131 us (33%)
  blocking collectives  85.5 us (21%)
  matrix products  81.5 us (20%)
  other arithmetic  52.2 us (13%)
  starting transfers between devices  23.7 us (6%)
  between operations  17 us (4%)
  local copies, waits for them, and re-layouts  6.76 us (2%)
    all_gather x1, waiting for transfers between devices, local(): key_piece = lax.all_gather(qkv[:, 1], 'seq', axis=0, tiled=True)  69.6 us
    all_to_all x2, blocking collectives, sent_to_all(): return lax.all_to_all(copies, axis, split_axis=0, concat_axis=0, tiled=True)  57.6 us
    dot_general x1, matrix products, local(): jnp.einsum('qhe,khe->hqk', query, key_heads, preferred_element_type=jnp.f...  30 us
    dot_general x1, matrix products, local(): jnp.einsum('hqk,khe->hqe', weights.astype(jnp.bfloat16), value_heads, pre...  28.9 us
    all_to_all x1, blocking collectives, summed_on_arrival(): blocks = lax.all_to_all(cut_along(array, dim, size), axis, 0, 0, tiled=True)  28 us
    all_gather x1, waiting for transfers between devices, local(): value_piece = lax.all_gather(qkv[:, 2], 'seq', axis=0, tiled=True)  25 us
    reduce_sum x1, other arithmetic, local(): total = jnp.sum(weights, axis=-1)  23.6 us
    all_to_all x1, waiting for transfers between devices, summed_on_arrival(): blocks = lax.all_to_all(cut_along(array, dim, size), axis, 0, 0, tiled=True)  22.3 us
  transfers between devices with their start and end apart: 6, of which 6 were waited for; matrix products, arithmetic and copies ran while one was open for 16% of the time, Pallas kernels for 0%

commit v1 on v0

--- a/solution.py
+++ b/solution.py
@@ -1,10 +1,397 @@
+import functools
+import math
+
 import jax
 import jax.numpy as jnp
 from jax import lax
+from jax.experimental import pallas as pl
+from jax.experimental.pallas import tpu as pltpu
 from jax.sharding import PartitionSpec as P
 
 HEAD_DIM = 128
 TOK_FRAME = 256
+ROWS = 128
+BLOCK = 512
+D = 2048
+BF16 = jnp.bfloat16
+F32 = jnp.float32
+MESH = pl.DeviceIdType.MESH
+QSCALE = math.log2(math.e) / math.sqrt(HEAD_DIM)
+NEG = -1e30
+
+
+def remote(src, dst, send_sem, recv_sem, where):
+    return pltpu.make_async_remote_copy(
+        src_ref=src, dst_ref=dst, send_sem=send_sem, recv_sem=recv_sem,
+        device_id=where, device_id_type=MESH,
+    )
+
+
+def al(i, m):
+    return pl.multiple_of(i, m)
+
+
+class Place:
+    def __init__(self):
+        self.c = lax.axis_index("dp")
+        s = lax.axis_index("seq")
+        self.s = s
+        self.z = lax.axis_index("tensor")
+        y, x = s // 4, s % 4
+        self.p = y * (1 - self.c) + x * self.c
+        self.g = x * (1 - self.c) + y * self.c
+
+    def seq(self, p, g):
+        return (p * 4 + g) * (1 - self.c) + (g * 4 + p) * self.c
+
+    def flip(self, p):
+        return (1 - self.c) * (1 - p % 2) + self.c * (p // 2)
+
+    def gq(self, p, g):
+        return g + self.flip(p) * (3 - 2 * g)
+
+
+def norm_rows(src, gain_ref, dst, rows):
+    def body(i, carry):
+        at = pl.ds(al(i * 16, 16), 16)
+        x = src[at, :].astype(F32)
+        square = jnp.mean(x * x, axis=-1, keepdims=True)
+        dst[at, :] = (x * lax.rsqrt(square + 1e-5) * gain_ref[...]).astype(BF16)
+        return carry
+
+    lax.fori_loop(0, rows // 16, body, 0)
+
+
+def attn_kernel(
+    vf_ref, tok_hbm, gain_ref, w_hbm, mixed_ref,
+    tok, w, normed, stage, qx, kx, vx, m_s, acc, o_stage,
+    tl_sem, w_sem, ts_sem, tr_sem, a_send, q_recv, k_recv, v_recv, qs_recv,
+    g_send, gk_recv, gv_recv, r_recv, o_send, o_recv,
+):
+    me = Place()
+    c, z, p, g = me.c, me.z, me.p, me.g
+    zp, zm, z2 = (z + 1) % 4, (z + 3) % 4, (z + 2) % 4
+    gp, gm, g2 = (g + 1) % 4, (g + 3) % 4, (g + 2) % 4
+    flip = me.flip(p)
+
+    own_in = pltpu.make_async_copy(tok_hbm, tok.at[z], tl_sem)
+    own_in.start()
+    w_in = [pltpu.make_async_copy(w_hbm.at[k], w.at[k], w_sem.at[k]) for k in range(3)]
+    for copy in w_in:
+        copy.start()
+
+    barrier = pltpu.get_barrier_semaphore()
+    for t in (zp, zm):
+        pl.semaphore_signal(barrier, inc=1, device_id={"tensor": t}, device_id_type=MESH)
+    for d in (1, 2, 3):
+        pl.semaphore_signal(barrier, inc=1, device_id={"seq": me.seq((p + d) % 4, g)}, device_id_type=MESH)
+    for d in range(4):
+        pl.semaphore_signal(barrier, inc=1, device_id={"seq": me.seq((p + d) % 4, 3 - g)}, device_id_type=MESH)
+    for k in (gp, gm):
+        pl.semaphore_signal(barrier, inc=1, device_id={"seq": me.seq(p, k)}, device_id_type=MESH)
+    own_in.wait()
+    pl.semaphore_wait(barrier, 11)
+
+    lo, hi = pl.ds(0, 64), pl.ds(64, 64)
+    halves = (lo, hi)
+    sends = []
+
+    def tok_send(direction, k, t, half):
+        to = zp if direction == 0 else zm
+        copy = remote(
+            tok.at[t, halves[half], :], tok.at[t, halves[half], :],
+            ts_sem.at[direction, k], tr_sem.at[direction, k], {"tensor": to},
+        )
+        copy.start()
+        sends.append(copy)
+
+    def tok_wait(direction, k, t, half):
+        remote(
+            tok.at[t, halves[half], :], tok.at[t, halves[half], :],
+            ts_sem.at[direction, k], tr_sem.at[direction, k], {"tensor": zp},
+        ).wait_recv()
+
+    tok_send(0, 0, z, 0)
+    tok_send(1, 0, z, 1)
+    tok_send(0, 1, z, 1)
+    tok_send(1, 1, z, 0)
+
+    def project(t):
+        norm_rows(tok.at[t], gain_ref, normed, ROWS)
+        for k in range(3):
+            for pair in range(2):
+                out = jnp.dot(
+                    normed[...], w[k, :, pair * 256 : pair * 256 + 256], preferred_element_type=F32
+                )
+                if k == 0:
+                    out = out * QSCALE
+                out = out.astype(BF16)
+                stage[t, 2 * pair, k] = out[:, :128]
+                stage[t, 2 * pair + 1, k] = out[:, 128:]
+
+    def hand_out(t):
+        rows = pl.ds(al(t * ROWS, ROWS), ROWS)
+        for d in (1, 2, 3):
+            h = (p + d) % 4
+            to_q = {"seq": me.seq(h, me.gq(p, g))}
+            to_kv = {"seq": me.seq(h, g)}
+            for k, (dst, sem, to) in enumerate(
+                (
+                    (qx.at[p, rows, pl.ds(0, 128)], q_recv.at[t], to_q),
+                    (kx.at[g * 4 + p, rows, pl.ds(0, 128)], k_recv.at[t], to_kv),
+                    (vx.at[g * 4 + p, rows, pl.ds(0, 128)], v_recv.at[t], to_kv),
+                )
+            ):
+                copy = remote(stage.at[t, h, k], dst, a_send.at[t, d - 1, k], sem, to)
+                copy.start()
+                sends.append(copy)
+        kx[g * 4 + p, rows, 0:128] = stage[t, p, 1]
+        vx[g * 4 + p, rows, 0:128] = stage[t, p, 2]
+
+        @pl.when(flip == 1)
+        def _():
+            remote(
+                stage.at[t, p, 0], qx.at[p, rows, pl.ds(0, 128)], a_send.at[t, 3, 0], qs_recv.at[t],
+                {"seq": me.seq(p, 3 - g)},
+            ).start()
+
+        @pl.when(flip == 0)
+        def _():
+            qx[p, rows, 0:128] = stage[t, p, 0]
+
+    three = pl.ds(0, 3)
+
+    def three_in(sem, buf, t):
+        rows = pl.ds(al(t * ROWS, ROWS), ROWS)
+        ref = buf.at[three, rows, pl.ds(0, 128)]
+        remote(ref, ref, sem, sem, {"tensor": zp}).wait_recv()
+
+    def group_ref(buf, gg, t):
+        return buf.at[pl.ds(gg * 4, 4), pl.ds(al(t * ROWS, ROWS), ROWS), pl.ds(0, 128)]
+
+    def ring_out(t):
+        three_in(k_recv.at[t], kx, t)
+        three_in(v_recv.at[t], vx, t)
+        for direction in (0, 1):
+            to = {"seq": me.seq(p, gp if direction == 0 else gm)}
+            pair = ((kx, gk_recv, 0), (vx, gv_recv, 1))
+            for buf, sem, k in pair if direction == 0 else pair[::-1]:
+                ref = group_ref(buf, g, t)
+                copy = remote(ref, ref, g_send.at[direction, t, k], sem.at[direction, t], to)
+                copy.start()
+                sends.append(copy)
+
+    def ring_wait(buf, sem, gg, t):
+        ref = group_ref(buf, gg, t)
+        remote(ref, ref, sem, sem, {"tensor": zp}).wait_recv()
+
+    def relay(t):
+        ring_wait(kx, gk_recv.at[0, t], gm, t)
+        ref = group_ref(kx, gm, t)
+        copy = remote(ref, ref, g_send.at[0, t, 2], r_recv.at[0, t], {"seq": me.seq(p, gp)})
+        copy.start()
+        sends.append(copy)
+        ring_wait(vx, gv_recv.at[1, t], gp, t)
+        ref = group_ref(vx, gp, t)
+        copy = remote(ref, ref, g_send.at[1, t, 2], r_recv.at[1, t], {"seq": me.seq(p, gm)})
+        copy.start()
+        sends.append(copy)
+
+    for copy in w_in:
+        copy.wait()
+    project(z)
+    hand_out(z)
+
+    length = vf_ref[c]
+    lane = lax.broadcasted_iota(jnp.int32, (BLOCK, 128), 1)
+    row = lax.broadcasted_iota(jnp.int32, (BLOCK, 128), 0)
+
+    def fill(slot, carry):
+        block = me.seq(slot % 4, slot // 4)
+        frame = 2 * block + row // TOK_FRAME
+        bias = jnp.where((lane == 0) & (frame >= length), NEG, 0.0)
+        mine = 0
+        for i in range(4):
+            mine = mine + (lane == 1 + i).astype(jnp.int32) * (
+                me.seq(i, me.gq(i, g)) == block
+            ).astype(jnp.int32)
+        bias = jnp.where((mine > 0) & (row >= TOK_FRAME), NEG, bias)
+        kx[slot, :, 128:256] = bias.astype(BF16)
+        vx[slot, :, 128:256] = jnp.ones((BLOCK, 128), BF16)
+        return carry
+
+    lax.fori_loop(0, 16, fill, 0)
+    for i in range(4):
+        on = (lane == 0) | ((lane == 1 + i) & (row < TOK_FRAME))
+        qx[i, :, 128:256] = jnp.where(on, 1.0, 0.0).astype(BF16)
+        m_s[i] = jnp.full((BLOCK, 128), -1e38, F32)
+        acc[i] = jnp.zeros((BLOCK, 256), F32)
+
+    tok_wait(0, 0, zm, 0)
+    tok_send(0, 2, zm, 0)
+    tok_wait(1, 0, zp, 1)
+    tok_send(1, 2, zp, 1)
+    ring_out(z)
+    tok_wait(0, 1, zm, 1)
+    project(zm)
+    hand_out(zm)
+    tok_wait(1, 1, zp, 0)
+    project(zp)
+    hand_out(zp)
+    relay(z)
+    ring_out(zm)
+    ring_out(zp)
+    tok_wait(0, 2, z2, 0)
+    tok_wait(1, 2, z2, 1)
+    project(z2)
+    hand_out(z2)
+    relay(zm)
+    relay(zp)
+    ring_out(z2)
+    for k in range(4):
+        t = (z + k) % 4
+        three_in(q_recv.at[t], qx, t)
+
+        @pl.when(flip == 1)
+        def _():
+            ref = qx.at[p, pl.ds(al(t * ROWS, ROWS), ROWS), pl.ds(0, 128)]
+            remote(ref, ref, qs_recv.at[t], qs_recv.at[t], {"tensor": zp}).wait_recv()
+
+    def group(gg):
+        def per_q(i, carry):
+            n = me.seq(i, me.gq(i, g))
+            first = me.seq(0, gg)
+            step = 4 * (1 - c) + c
+            count = jnp.clip((n - first + step) // step, 0, 4)
+
+            def pair(j, carry):
+                slot = gg * 4 + j
+                for a in range(2):
+                    at = pl.ds(a * 256, 256)
+                    s = lax.dot_general(
+                        qx[i, at, :], kx[slot], (((1,), (1,)), ((), ())), preferred_element_type=F32
+                    )
+                    before = m_s[i, at, :]
+                    after = jnp.maximum(before, jnp.max(s, axis=1, keepdims=True))
+                    weights = jnp.exp2(s - after[:, :1]).astype(BF16)
+                    keep = jnp.exp2(before - after)
+                    m_s[i, at, :] = after
+                    acc[i, at, :] = acc[i, at, :] * jnp.concatenate([keep, keep], axis=1) + jnp.dot(
+                        weights, vx[slot], preferred_element_type=F32
+                    )
+                return carry
+
+            lax.fori_loop(0, count, pair, 0)
+            return carry
+
+        lax.fori_loop(0, 4, per_q, 0)
+
+    group(g)
+    relay(z2)
+    for k in range(4):
+        ring_wait(vx, gv_recv.at[0, (z + k) % 4], gm, (z + k) % 4)
+    group(gm)
+    for k in range(4):
+        ring_wait(kx, gk_recv.at[1, (z + k) % 4], gp, (z + k) % 4)
+    group(gp)
+    for k in range(4):
+        ring_wait(kx, r_recv.at[0, (z + k) % 4], g2, (z + k) % 4)
+        ring_wait(vx, r_recv.at[1, (z + k) % 4], g2, (z + k) % 4)
+    group(g2)
+
+    def finish(i):
+        o_stage[i] = (acc[i, :, 0:128] / acc[i, :, 128:256]).astype(BF16)
+
+    for d in (1, 2, 3):
+        i = (p + d) % 4
+        finish(i)
+        copy = remote(
+            o_stage.at[i], mixed_ref.at[p], o_send.at[d - 1], o_recv.at[p],
+            {"seq": me.seq(i, me.gq(i, g))},
+        )
+        copy.start()
+        sends.append(copy)
+    finish(p)
+
+    @pl.when(flip == 1)
+    def _():
+        remote(
+            o_stage.at[p], mixed_ref.at[p], o_send.at[3], o_recv.at[p], {"seq": me.seq(p, 3 - g)}
+        ).start()
+
+    @pl.when(flip == 0)
+    def _():
+        mixed_ref[p] = o_stage[p]
+
+    for d in (1, 2, 3):
+        h = (p + d) % 4
+        remote(o_stage.at[0], mixed_ref.at[h], o_send.at[0], o_recv.at[h], {"tensor": zp}).wait_recv()
+
+    @pl.when(flip == 1)
+    def _():
+        back = remote(
+            o_stage.at[p], mixed_ref.at[p], o_send.at[3], o_recv.at[p], {"seq": me.seq(p, 3 - g)}
+        )
+        back.wait_recv()
+        back.wait_send()
+        for t in range(4):
+            rows = pl.ds(t * ROWS, ROWS)
+            remote(
+                stage.at[t, p, 0], qx.at[p, rows, pl.ds(0, 128)], a_send.at[t, 3, 0], qs_recv.at[t],
+                {"seq": me.seq(p, 3 - g)},
+            ).wait_send()
+
+    for copy in sends:
+        copy.wait_send()
+
+
+def attention(tokens, gain, w_qkv, lengths):
+    vmem = pltpu.VMEM
+    dma = pltpu.SemaphoreType.DMA
+    return pl.pallas_call(
+        attn_kernel,
+        out_shape=jax.ShapeDtypeStruct((4, BLOCK, HEAD_DIM), BF16),
+        in_specs=[
+            pl.BlockSpec(memory_space=pltpu.SMEM),
+            pl.BlockSpec(memory_space=pl.ANY),
+            pl.BlockSpec(memory_space=pltpu.VMEM),
+            pl.BlockSpec(memory_space=pl.ANY),
+        ],
+        out_specs=pl.BlockSpec(memory_space=pltpu.VMEM),
+        scratch_shapes=[
+            vmem((4, ROWS, D), BF16),
+            vmem((3, D, BLOCK), BF16),
+            vmem((ROWS, D), BF16),
+            vmem((4, 4, 3, ROWS, HEAD_DIM), BF16),
+            vmem((4, BLOCK, 256), BF16),
+            vmem((16, BLOCK, 256), BF16),
+            vmem((16, BLOCK, 256), BF16),
+            vmem((4, BLOCK, 128), F32),
+            vmem((4, BLOCK, 256), F32),
+            vmem((4, BLOCK, HEAD_DIM), BF16),
+            dma,
+            dma((3,)),
+            dma((2, 3)),
+            dma((2, 3)),
+            dma((4, 4, 3)),
+            dma((4,)),
+            dma((4,)),
+            dma((4,)),
+            dma((4,)),
+            dma((2, 4, 3)),
+            dma((2, 4)),
+            dma((2, 4)),
+            dma((2, 4)),
+            dma((4,)),
+            dma((4,)),
+        ],
+        compiler_params=pltpu.CompilerParams(
+            collective_id=0, has_side_effects=True, vmem_limit_bytes=52 * 2**20
+        ),
+        cost_estimate=pl.CostEstimate(flops=2 * 10**10, bytes_accessed=2 * 10**7, transcendentals=10**7),
+    )(lengths, tokens, gain.reshape(1, D), w_qkv)
+
+
 FR_DEV = 2
 
 
@@ -108,46 +495,8 @@
     tensor_index = lax.axis_index("tensor")
     roll_index = lax.axis_index("dp")
     length = valid_frames[roll_index]
-    local_heads = w_qkv.shape[2] // HEAD_DIM
-    scale = 1.0 / HEAD_DIM**0.5
-    normed = rms_norm(rows, attn_gain)
-    qkv = jnp.einsum(
-        "nd,cde->nce",
-        gathered_copies(normed, "tensor", 0),
-        w_qkv,
-        preferred_element_type=jnp.float32,
-    ).astype(jnp.bfloat16)
-    block = qkv.shape[0]
-    query = qkv[:, 0].reshape(block, local_heads, HEAD_DIM)
-    query_frame = (seq_index * block + jnp.arange(block, dtype=jnp.int32)) // TOK_FRAME
-    peak = jnp.full((local_heads, block), -1e30, jnp.float32)
-    key_piece = lax.all_gather(qkv[:, 1], "seq", axis=0, tiled=True)
-    value_piece = lax.all_gather(qkv[:, 2], "seq", axis=0, tiled=True)
-    width = key_piece.shape[0]
-    key_heads = key_piece.reshape(width, local_heads, HEAD_DIM)
-    value_heads = value_piece.reshape(width, local_heads, HEAD_DIM)
-    scores = (
-        jnp.einsum("qhe,khe->hqk", query, key_heads, preferred_element_type=jnp.float32) * scale
-    )
-    key_frame = jnp.arange(width, dtype=jnp.int32) // TOK_FRAME
-    allowed = (key_frame[None, :] <= query_frame[:, None]) & (key_frame[None, :] < length)
-    scores = jnp.where(allowed[None], scores, -1e30)
-    new_peak = jnp.maximum(peak, jnp.max(scores, axis=-1))
-    weights = jnp.where(allowed[None], jnp.exp(scores - new_peak[..., None]), 0.0)
-    total = jnp.sum(weights, axis=-1)
-    acc = jnp.einsum(
-        "hqk,khe->hqe",
-        weights.astype(jnp.bfloat16),
-        value_heads,
-        preferred_element_type=jnp.float32,
-    )
-    peak, total, acc = (new_peak, total, acc)
-    mixed = (
-        (acc / total[..., None])
-        .transpose(1, 0, 2)
-        .reshape(block, local_heads * HEAD_DIM)
-        .astype(jnp.bfloat16)
-    )
+    heads = attention(rows, attn_gain, w_qkv, valid_frames)
+    mixed = heads.transpose(1, 0, 2).reshape(BLOCK, 4 * HEAD_DIM)
     attn_sum = summed_on_arrival(
         jnp.dot(mixed, w_out, preferred_element_type=jnp.float32).astype(jnp.bfloat16), "tensor", 0
     )

time: 399 us -> 252 us (0.63)
  waiting for transfers between devices: 131 us -> 30.3 us
  Pallas kernels: 0 us -> 81.2 us
  matrix products: 81.5 us -> 18.1 us
  blocking collectives: 85.5 us -> 43.2 us
  other arithmetic: 52.2 us -> 16.4 us
  starting transfers between devices: 23.7 us -> 50.8 us
  between operations: 17 us -> 3.6 us
    all_gather x2 -> x0, waiting for transfers between devices: 94.6 us -> none  [the longest x1 69.6 us: local(): key_piece = lax.all_gather(qkv[:, 1], 'seq', axis=0, tiled=True)]
    pallas_call x0 -> x1, Pallas kernels: none -> 81.2 us  [attention(): pl.pallas_call(attn_kernel, out_shape=jax.ShapeDtypeStruct((4, BLOCK, HEA...]
    dot_general x3 -> x0, matrix products: 62.4 us -> none  [the longest x1 30 us: local(): jnp.einsum('qhe,khe->hqk', query, key_heads, preferred_element_type=jnp.f...]
    all_to_all x2 -> x1, blocking collectives: 57.6 us -> 21.5 us  [sent_to_all(): return lax.all_to_all(copies, axis, split_axis=0, concat_axis=0, tiled=True)]
    all_to_all x3, starting transfers between devices: 19.1 us -> 46.2 us  [sent_to_all(): return lax.all_to_all(copies, axis, split_axis=0, concat_axis=0, tiled=True)]
    reduce_sum x1 -> x0, other arithmetic: 23.6 us -> none  [local(): total = jnp.sum(weights, axis=-1)]
    all_to_all x1, blocking collectives: 28 us -> 21.7 us  [summed_on_arrival(): blocks = lax.all_to_all(cut_along(array, dim, size), axis, 0, 0, tiled=True)]
    all_to_all x1, waiting for transfers between devices: 22.3 us -> 16.5 us  [summed_on_arrival(): blocks = lax.all_to_all(cut_along(array, dim, size), axis, 0, 0, tiled=True)]
  transfers between devices with their start and end apart: 6 -> 4, of which waited for: 6 -> 4; matrix products, arithmetic and copies ran while one was open for 16% -> 2% of each run, Pallas kernels for 0% -> 0%
where the time goes in v1:
time: 252 us; the launch traced here: 251 us
  Pallas kernels  81.2 us (32%)
  starting transfers between devices  50.8 us (20%)
  blocking collectives  43.2 us (17%)
  waiting for transfers between devices  30.3 us (12%)
  matrix products  18.1 us (7%)
  other arithmetic  16.4 us (7%)
  local copies, waits for them, and re-layouts  7.44 us (3%)
  between operations  3.6 us (1%)
    pallas_call x1, Pallas kernels, attention(): pl.pallas_call(attn_kernel, out_shape=jax.ShapeDtypeStruct((4, BLOCK, HEA...  81.2 us
    all_to_all x3, starting transfers between devices, sent_to_all(): return lax.all_to_all(copies, axis, split_axis=0, concat_axis=0, tiled=True)  46.2 us
    all_to_all x1, blocking collectives, summed_on_arrival(): blocks = lax.all_to_all(cut_along(array, dim, size), axis, 0, 0, tiled=True)  21.7 us
    all_to_all x1, blocking collectives, sent_to_all(): return lax.all_to_all(copies, axis, split_axis=0, concat_axis=0, tiled=True)  21.5 us
    dot_general x1, matrix products, local(): jnp.dot(up, w_down, preferred_element_type=jnp.float32).astype(jnp.bfloat16)  16.6 us
    all_to_all x1, waiting for transfers between devices, summed_on_arrival(): blocks = lax.all_to_all(cut_along(array, dim, size), axis, 0, 0, tiled=True)  16.5 us
    all_to_all x3, waiting for transfers between devices, sent_to_all(): return lax.all_to_all(copies, axis, split_axis=0, concat_axis=0, tiled=True)  13.9 us
  transfers between devices with their start and end apart: 4, of which 4 were waited for; matrix products, arithmetic and copies ran while one was open for 2% of the time, Pallas kernels for 0%

profile of v1, /device:TPU:1, one launch (start us, length us, event | category | flops | bytes accessed | tf_op | source)
XLA Modules:
  0.0 251.1 jit_solution(12863808670916055834)
XLA Ops:
  0.7 1.2 copy-done.1
  2.5 0.7 copy-done.5
  3.2 81.2 %shard_map.130 = bf16[4,512,128]{2,1,0:T(8,128)(2,1)S(1)} custom-call(s32[2]{0:T(128)S(1)} %copy-done.3, bf16[128,2048]{1,0:T(8,128)(2,1)S(1)} %bitcast.43, f32[1,2048]{1,0:T(1,128)S(1)} %bitcast.45, bf16[3,2048,512]{2,1,0:T(8,128)(2,1)} %w_hbm.1), custom_call_target="tpu_custom_call" | custom-call | flops 20000000000 | bytes 20000000 | tf_op jit(solution)/shard_map/pallas_call | solution.py:351
  84.7 1.3 convolution_convert_fusion.1
  86.0 21.7 %all_to_all.30 = bf16[4,128,2048]{2,1,0:T(8,128)(2,1)S(1)} all-to-all(bf16[4,128,2048]{2,1,0:T(8,128)(2,1)S(1)} %bitcast.47), channel_id=1, replica_groups=mesh['dp'=2,'seq'=16,'tensor'=4] {'tensor'}, dimensions={0} | all-to-all | bytes 4194304 | tf_op jit(solution)/shard_map/all_to_all | solution.py:421
  108.8 21.5 %all_to_all.31 = bf16[4,128,2048]{2,1,0:T(8,128)(2,1)} all-to-all(bf16[4,128,2048]{2,1,0:T(8,128)(2,1)S(1)} %broadcast_in_dim.70), channel_id=1, replica_groups=mesh['dp'=2,'seq'=16,'tensor'=4] {'tensor'}, dimensions={0} | all-to-all | bytes 4194304 | tf_op jit(solution)/shard_map/all_to_all | solution.py:406
  130.3 16.6 %convolution_convert_fusion = bf16[512,2048]{1,0:T(8,128)(2,1)} fusion(bf16[2048,2048]{1,0:T(8,128)(2,1)} %param.17, bf16[512,2048]{1,0:T(8,128)(2,1)} %bitcast.48, bf16[2048,2048]{1,0:T(8,128)(2,1)} %param.16), kind=kOutput, calls=%fused_computation.11 | convolution fusion | flops 8600420352 | bytes 20971520 | tf_op jit(solution)/shard_map/dot_general | solution.py:510
  146.9 4.6 %all-to-all-start.2 = ((bf16[4,128,2048]{2,1,0:T(8,128)(2,1)}), bf16[4,128,2048]{2,1,0:T(8,128)(2,1)}, u32[]{:S(2)}, u32[]{:S(2)}) async-start(bf16[4,128,2048]{2,1,0:T(8,128)(2,1)} %bitcast.46), calls=%async_computation.2 | async-start | bytes 4194304 | tf_op jit(solution)/shard_map/all_to_all | solution.py:421
  152.1 16.5 %all-to-all-done.2 = bf16[4,128,2048]{2,1,0:T(8,128)(2,1)} async-done(((bf16[4,128,2048]{2,1,0:T(8,128)(2,1)}), bf16[4,128,2048]{2,1,0:T(8,128)(2,1)}, u32[]{:S(2)}, u32[]{:S(2)}) %all-to-all-start.2) | async-done | bytes 2097184 | tf_op jit(solution)/shard_map/all_to_all | solution.py:421
  168.6 2.1 convert_reduce_fusion
  170.7 1.0 copy-done.7
  172.6 3.3 %all-to-all-start.3 = ((f32[4,2,2048]{2,1,0:T(2,128)}), f32[4,2,2048]{2,1,0:T(2,128)S(1)}, u32[]{:S(2)}, u32[]{:S(2)}) async-start(f32[4,2,2048]{2,1,0:T(2,128)} %broadcast_in_dim.72), calls=%async_computation.3 | async-start | bytes 131072 | tf_op jit(solution)/shard_map/all_to_all | solution.py:406
  176.5 3.8 %all-to-all-done.3 = f32[4,2,2048]{2,1,0:T(2,128)S(1)} async-done(((f32[4,2,2048]{2,1,0:T(2,128)}), f32[4,2,2048]{2,1,0:T(2,128)S(1)}, u32[]{:S(2)}, u32[]{:S(2)}) %all-to-all-start.3) | async-done | bytes 65568 | tf_op jit(solution)/shard_map/all_to_all | solution.py:406
  180.6 0.8 broadcast_in_dim.75
  181.4 34.7 %all-to-all-start.4 = ((f32[16,2,2048]{2,1,0:T(2,128)}), f32[16,2,2048]{2,1,0:T(2,128)S(1)}, u32[]{:S(2)}, u32[]{:S(2)}) async-start(f32[16,2,2048]{2,1,0:T(2,128)} %broadcast_in_dim.75), calls=%async_computation.4 | async-start | bytes 524288 | tf_op jit(solution)/shard_map/all_to_all | solution.py:406
  218.0 5.6 %all-to-all-done.4 = f32[16,2,2048]{2,1,0:T(2,128)S(1)} async-done(((f32[16,2,2048]{2,1,0:T(2,128)}), f32[16,2,2048]{2,1,0:T(2,128)S(1)}, u32[]{:S(2)}, u32[]{:S(2)}) %all-to-all-start.4) | async-done | bytes 262176 | tf_op jit(solution)/shard_map/all_to_all | solution.py:406
  224.4 0.7 multiply_reduce_fusion.1
  225.1 2.6 %fusion.28 = (f32[]{:T(128)}, f32[]{:T(128)}, f32[]{:T(128)}) fusion(s32[]{:T(128)S(6)} %sub.49, s32[]{:T(128)S(6)} %mul.167, f32[1]{0:T(128)} %bitcast.18, f32[1]{0:T(128)} %bitcast.17, s32[]{:T(128)} %bitcast.9), kind=kLoop, calls=%fused_computation.63 | loop fusion | flops 17 | bytes 32 | tf_op jit(solution)/shard_map/reduce_sum | solution.py:543
  227.7 2.0 pad_maximum_fusion.1
  230.4 8.3 %all-to-all-start.5 = ((f32[32,3,2]{1,2,0:T(2,128)}), f32[32,3,2]{1,2,0:T(2,128)S(1)}, u32[]{:S(2)}, u32[]{:S(2)}) async-start(f32[32,3,2]{1,2,0:T(2,128)} %broadcast_in_dim.80), calls=%async_computation.5 | async-start | bytes 65536 | tf_op jit(solution)/shard_map/all_to_all | solution.py:406
  238.7 2.5 fusion.17
  241.2 4.5 %all-to-all-done.5 = f32[32,3,2]{1,2,0:T(2,128)S(1)} async-done(((f32[32,3,2]{1,2,0:T(2,128)}), f32[32,3,2]{1,2,0:T(2,128)S(1)}, u32[]{:S(2)}, u32[]{:S(2)}) %all-to-all-start.5) | async-done | bytes 800 | tf_op jit(solution)/shard_map/all_to_all | solution.py:406
  245.9 0.7 subtract_reduce_fusion
  247.9 3.2 %multiply_select_fusion.1 = (f32[1,2]{1,0:T(1,128)}, f32[1,2]{1,0:T(1,128)}) fusion(f32[]{:T(128)S(6)} %rsqrt.12, f32[]{:T(128)S(6)} %div.42, f32[]{:T(128)} %get-tuple-element.10, s32[]{:T(128)} %bitcast.9, s32[]{:T(128)S(6)} %mul.167, f32[1,1]{1,0:T(1,128)} %bitcast.16, f32[1,1]{1,0:T(1,128)} %bitcast.13), kind=kLoop, calls=%fused_computation.67 | loop fusion | flops 20 | bytes 44 | tf_op jit(solution)/shard_map/jit(_where)/select_n | solution.py:556
  (63 shorter events, 6.7 us)
Async XLA Ops:
  0.6 84.0 %copy-start = (bf16[512,2048]{1,0:T(8,128)(2,1)S(1)}, bf16[512,2048]{1,0:T(8,128)(2,1)}, u32[]{:S(2)}) copy-start(bf16[512,2048]{1,0:T(8,128)(2,1)} %param.14) | copy-start | bytes 6291460
  0.6 1.2 copy-start.1
  1.8 0.7 copy-start.3
  2.5 0.7 copy-start.5
  86.0 22.1 %copy-start.2 = (bf16[1,128,2048]{2,1,0:T(8,128)(2,1)S(1)}, bf16[1,128,2048]{2,1,0:T(8,128)(2,1)}, u32[]{:S(2)}) copy-start(bf16[1,128,2048]{2,1,0:T(8,128)(2,1)} %param.11) | copy-start | bytes 1572868
  86.0 22.4 %copy-start.8 = (f32[2048]{0:T(1024)S(1)}, f32[2048]{0:T(1024)}, u32[]{:S(2)}) copy-start(f32[2048]{0:T(1024)} %param.15) | copy-start | bytes 24580
  108.1 22.2 %copy-start.6 = (f32[128,2048]{1,0:T(8,128)}, f32[128,2048]{1,0:T(8,128)S(1)}, u32[]{:S(2)}) copy-start(f32[128,2048]{1,0:T(8,128)S(1)} %convert_reduce_fusion.1) | copy-start | bytes 3145732
  146.9 4.6 %copy-start.4 = (s32[2]{0:T(128)S(1)}, s32[2]{0:T(128)}, u32[]{:S(2)}) copy-start(s32[2]{0:T(128)} %vf_ref.1) | copy-start | bytes 28
  146.9 5.2 %copy-start.9 = (f32[2048]{0:T(1024)S(1)}, f32[2048]{0:T(1024)}, u32[]{:S(2)}) copy-start(f32[2048]{0:T(1024)} %param.18) | copy-start | bytes 24580
  146.9 33.5 %copy-start.11 = (f32[2048]{0:T(1024)S(1)}, f32[2048]{0:T(1024)}, u32[]{:S(2)}) copy-start(f32[2048]{0:T(1024)} %param.19) | copy-start | bytes 24580
  146.9 21.7 %all-to-all-start.2 = ((bf16[4,128,2048]{2,1,0:T(8,128)(2,1)}), bf16[4,128,2048]{2,1,0:T(8,128)(2,1)}, u32[]{:S(2)}, u32[]{:S(2)}) async-start(bf16[4,128,2048]{2,1,0:T(8,128)(2,1)} %bitcast.46), calls=%async_computation.2 | async-start | bytes 4194304 | tf_op jit(solution)/shard_map/all_to_all | solution.py:421
  152.1 72.3 %copy-start.10 = (f32[2048]{0:T(1024)S(1)}, f32[2048]{0:T(1024)}, u32[]{:S(2)}) copy-start(f32[2048]{0:T(1024)} %param.20) | copy-start | bytes 24580
  170.7 1.0 copy-start.7
  172.6 7.7 %all-to-all-start.3 = ((f32[4,2,2048]{2,1,0:T(2,128)}), f32[4,2,2048]{2,1,0:T(2,128)S(1)}, u32[]{:S(2)}, u32[]{:S(2)}) async-start(f32[4,2,2048]{2,1,0:T(2,128)} %broadcast_in_dim.72), calls=%async_computation.3 | async-start | bytes 131072 | tf_op jit(solution)/shard_map/all_to_all | solution.py:406
  181.4 42.2 %all-to-all-start.4 = ((f32[16,2,2048]{2,1,0:T(2,128)}), f32[16,2,2048]{2,1,0:T(2,128)S(1)}, u32[]{:S(2)}, u32[]{:S(2)}) async-start(f32[16,2,2048]{2,1,0:T(2,128)} %broadcast_in_dim.75), calls=%async_computation.4 | async-start | bytes 524288 | tf_op jit(solution)/shard_map/all_to_all | solution.py:406
  230.4 15.3 %all-to-all-start.5 = ((f32[32,3,2]{1,2,0:T(2,128)}), f32[32,3,2]{1,2,0:T(2,128)S(1)}, u32[]{:S(2)}, u32[]{:S(2)}) async-start(f32[32,3,2]{1,2,0:T(2,128)} %broadcast_in_dim.80), calls=%async_computation.5 | async-start | bytes 65536 | tf_op jit(solution)/shard_map/all_to_all | solution.py:406

commit v2 on v1

--- a/solution.py
+++ b/solution.py
@@ -392,169 +392,303 @@
     )(lengths, tokens, gain.reshape(1, D), w_qkv)
 
 
-FR_DEV = 2
-
-
-def laid_out(blocks, dim):
-    shape = list(blocks.shape[1:])
-    shape[dim] *= blocks.shape[0]
-    return jnp.moveaxis(blocks, 0, dim).reshape(shape)
-
-
-def sent_to_all(array, axis):
-    copies = jnp.broadcast_to(array, (lax.axis_size(axis), *array.shape))
-    return lax.all_to_all(copies, axis, split_axis=0, concat_axis=0, tiled=True)
-
-
-def gathered_copies(array, axis, dim):
-    return laid_out(sent_to_all(array, axis), dim)
-
-
-def cut_along(array, dim, size):
-    shape = array.shape
-    blocks = array.reshape(*shape[:dim], size, shape[dim] // size, *shape[dim + 1 :])
-    return jnp.moveaxis(blocks, dim, 0)
-
-
-def summed_on_arrival(array, axis, dim):
-    size = lax.axis_size(axis)
-    blocks = lax.all_to_all(cut_along(array, dim, size), axis, 0, 0, tiled=True)
-    return jnp.sum(blocks.astype(jnp.float32), axis=0)
-
-
-def over_copies(array, axis):
-    everything = sent_to_all(array, axis)
-    return jnp.sum(everything, axis=0)
-
-
-def collected_together(array, axis):
-    leaves = jax.tree.leaves(array)
-    sequence = sorted(range(len(leaves)), key=lambda k: -leaves[k].size)
-    width = (1, *leaves[sequence[0]].shape)[-1]
-    lines = [
-        jnp.pad(leaves[k].reshape(-1), (0, -leaves[k].size % width)).reshape(-1, width)
-        for k in sequence
+def gelu(x):
+    return 0.5 * x * (1.0 + jnp.tanh(math.sqrt(2.0 / math.pi) * (x + 0.044715 * (x * x * x))))
+
+
+def mlp_kernel(
+    vf_ref, mixed_ref, tok_ref, gain_ref, pg_ref, pb_ref, vw_ref, wo_hbm, wu_hbm, wd_hbm,
+    hid_ref, fv_ref, adv_ref,
+    wo, wu, wd, part, mid, fin, nrm, after, own, up, fs, zs, means, states, vals,
+    w_sem, rs_send, mid_recv, fin_recv, ag_send, ag_recv, z_send, z_recv, s_send, s_recv, v_sem,
+):
+    c, s, z = lax.axis_index("dp"), lax.axis_index("seq"), lax.axis_index("tensor")
+    zp, zm, z2 = (z + 1) % 4, (z + 3) % 4, (z + 2) % 4
+    w_in = [
+        pltpu.make_async_copy(src, dst, w_sem.at[k])
+        for k, (src, dst) in enumerate(((wo_hbm, wo), (wu_hbm, wu), (wd_hbm, wd)))
     ]
-    both, at, found = (sent_to_all(jnp.concatenate(lines), axis), 0, {})
-    for k, line in zip(sequence, lines):
-        piece = both[:, at : at + len(line)].reshape(len(both), -1)
-        found[k] = piece[:, : leaves[k].size].reshape(-1, *leaves[k].shape)
-        at += len(line)
-    numbers = iter(range(len(leaves)))
-    return jax.tree.map(lambda _: found[next(numbers)], array)
-
-
-def combined_pairwise(pieces, combine):
-    while len(jax.tree.leaves(pieces)[0]) > 1:
-        pieces = jax.vmap(combine)(
-            *(jax.tree.map(lambda part: part[side::2], pieces) for side in (0, 1))
-        )
-    return jax.tree.map(lambda part: part[0], pieces)
-
-
-def entering_2(array, axis, combine, identity):
-    size, index = (lax.axis_size(axis), lax.axis_index(axis))
-    passed = jnp.arange(size) < index
-
-    def kept(part, zero, own):
-        part = jnp.where(
-            passed.reshape(-1, *(1 for _ in own.shape)), part, jnp.asarray(zero, own.dtype)
-        )
-        return part
-
-    pieces = collected_together(array, axis)
-    return combined_pairwise(jax.tree.map(kept, pieces, identity, array), combine)
-
-
-def rms_norm(values, gain):
-    floats = values.astype(jnp.float32)
-    square = jnp.mean(floats * floats, axis=-1, keepdims=True)
-    return (floats * lax.rsqrt(square + 1e-05) * gain).astype(jnp.bfloat16)
-
-
-def compose(earlier, later):
-    return (earlier[0] * later[0], later[0] * earlier[1] + later[1])
+    for copy in w_in:
+        copy.start()
+    barrier = pltpu.get_barrier_semaphore()
+    for t in (zp, zm, z2):
+        pl.semaphore_signal(barrier, inc=1, device_id={"tensor": t}, device_id_type=MESH)
+    for d in range(1, 16):
+        pl.semaphore_signal(barrier, inc=1, device_id={"seq": (s + d) % 16}, device_id_type=MESH)
+    pl.semaphore_signal(barrier, inc=1, device_id={"dp": 1 - c}, device_id_type=MESH)
+
+    lo, hi = pl.ds(0, 64), pl.ds(64, 64)
+    sends = []
+
+    def send(src, dst, send_sem, recv_sem, to):
+        copy = remote(src, dst, send_sem, recv_sem, to)
+        copy.start()
+        sends.append(copy)
+
+    def arrive(ref, sem):
+        remote(ref, ref, sem, sem, {"tensor": zp}).wait_recv()
+
+    def out_project(t):
+        rows = pl.ds(al(t * ROWS, ROWS), ROWS)
+        lhs = jnp.concatenate([mixed_ref[h, rows, :] for h in range(4)], axis=1)
+        for n in range(4):
+            cols = slice(n * 512, n * 512 + 512)
+            part[0, t, :, cols] = jnp.dot(lhs, wo[:, cols], preferred_element_type=F32).astype(BF16)
+
+    def send_mids(k):
+        send(part.at[k, z2, lo, :], mid.at[k, 0], rs_send.at[k, 0], mid_recv.at[k, 0], {"tensor": zp})
+        send(part.at[k, z2, hi, :], mid.at[k, 1], rs_send.at[k, 1], mid_recv.at[k, 1], {"tensor": zm})
+
+    def send_direct(k):
+        send(part.at[k, zp, hi, :], fin.at[k, 0, hi, :], rs_send.at[k, 2], fin_recv.at[k, 0, 1], {"tensor": zp})
+        send(part.at[k, zm, lo, :], fin.at[k, 1, lo, :], rs_send.at[k, 3], fin_recv.at[k, 1, 0], {"tensor": zm})
+
+    def send_sums(k):
+        for direction, (t, half) in enumerate(((zp, 0), (zm, 64))):
+            arrive(mid.at[k, direction], mid_recv.at[k, direction])
+
+            def add(i, carry):
+                at = pl.ds(al(i * 16, 16), 16)
+                to = pl.ds(al(half + i * 16, 16), 16)
+                part[k, t, to, :] = (part[k, t, to, :].astype(F32) + mid[k, direction, at, :].astype(F32)).astype(BF16)
+                return carry
+
+            lax.fori_loop(0, 4, add, 0)
+            rows = pl.ds(half, 64)
+            send(
+                part.at[k, t, rows, :], fin.at[k, direction, rows, :], rs_send.at[k, 4 + direction],
+                fin_recv.at[k, direction, direction], {"tensor": t},
+            )
+
+    def wait_final(k):
+        for direction in (0, 1):
+            for half, rows in enumerate((lo, hi)):
+                arrive(fin.at[k, direction, rows, :], fin_recv.at[k, direction, half])
+
+    w_in[0].wait()
+    out_project(z2)
+    pl.semaphore_wait(barrier, 19)
+    send_mids(0)
+    out_project(zp)
+    out_project(zm)
+    send_direct(0)
+    out_project(z)
+    send_sums(0)
+    wait_final(0)
+
+    def settle(i, carry):
+        at = pl.ds(al(i * 16, 16), 16)
+        total = part[0, z, at, :].astype(F32) + fin[0, 0, at, :].astype(F32) + fin[0, 1, at, :].astype(F32)
+        x = (tok_ref[at, :].astype(F32) + total).astype(BF16)
+        after[at, :] = x
+        x = x.astype(F32)
+        square = jnp.mean(x * x, axis=-1, keepdims=True)
+        nrm[z, at, :] = (x * lax.rsqrt(square + 1e-5) * gain_ref[...]).astype(BF16)
+        return carry
+
+    lax.fori_loop(0, 8, settle, 0)
+
+    halves = (lo, hi)
+
+    def ring_send(direction, k, t, half):
+        ref = nrm.at[t, halves[half], :]
+        send(ref, ref, ag_send.at[direction, k], ag_recv.at[direction, k], {"tensor": zp if direction == 0 else zm})
+
+    def ring_wait(direction, k, t, half):
+        arrive(nrm.at[t, halves[half], :], ag_recv.at[direction, k])
+
+    ring_send(0, 0, z, 0)
+    ring_send(1, 0, z, 1)
+    ring_send(0, 1, z, 1)
+    ring_send(1, 1, z, 0)
+
+    for k in (0, 1):
+        fs[k] = jnp.zeros((8, D), F32)
+
+    def up_down(ts, keep):
+        rows = ROWS * len(ts)
+
+        def up_step(n, carry):
+            cols = pl.ds(al(n * 256, 256), 256)
+            lhs = jnp.concatenate([nrm[t] for t in ts], axis=0) if len(ts) > 1 else nrm[ts[0]]
+            x = jnp.dot(lhs, wu[:, cols], preferred_element_type=F32)
+            up[0:rows, cols] = gelu(x).astype(BF16)
+            return carry
+
+        lax.fori_loop(0, 8, up_step, 0)
+
+        def down_step(n, carry):
+            cols = pl.ds(al(n * 256, 256), 256)
+            x = jnp.dot(up[0:rows, :], wd[:, cols], preferred_element_type=F32)
+            for k, t in enumerate(ts):
+                y = x[k * ROWS : (k + 1) * ROWS]
+                fs[t // 2, :, cols] += jnp.sum(y.reshape(16, 8, 256), axis=0)
+                if keep:
+                    own[:, cols] = y
+                else:
+                    part[1, t, :, cols] = y.astype(BF16)
+            return carry
+
+        lax.fori_loop(0, 8, down_step, 0)
+
+    w_in[1].wait()
+    w_in[2].wait()
+    up_down((z,), True)
+    ring_wait(0, 0, zm, 0)
+    ring_send(0, 2, zm, 0)
+    ring_wait(1, 0, zp, 1)
+    ring_send(1, 2, zp, 1)
+
+    def residual(i, carry):
+        at = pl.ds(al(i * 16, 16), 16)
+        fs[z // 2] += jnp.sum(after[at, :].astype(F32).reshape(2, 8, D), axis=0)
+        return carry
+
+    lax.fori_loop(0, 8, residual, 0)
+    ring_wait(0, 1, zm, 1)
+    ring_wait(1, 1, zp, 0)
+    up_down((zm, zp), False)
+    send_direct(1)
+    ring_wait(0, 2, z2, 0)
+    ring_wait(1, 2, z2, 1)
+    up_down((z2,), False)
+
+    for k in (0, 1):
+        zs[z, k : k + 1, :] = jnp.sum(fs[k], axis=0, keepdims=True)
+    for d in (1, 2, 3):
+        send(zs.at[z], zs.at[z], z_send.at[d - 1], z_recv.at[z], {"tensor": (z + d) % 4})
+    send_mids(1)
+    for d in (1, 2, 3):
+        t = (z + d) % 4
+        arrive(zs.at[t], z_recv.at[t])
+    means[s] = (zs[0] + zs[1] + zs[2] + zs[3]) * (1.0 / TOK_FRAME)
+    for d in range(1, 16):
+        send(means.at[s], means.at[s], s_send.at[d - 1], s_recv.at[s], {"seq": (s + d) % 16})
+    send_sums(1)
+
+    for d in range(1, 16):
+        t = (s + d) % 16
+        arrive(means.at[t], s_recv.at[t])
+    length = vf_ref[c]
+    frame = 2 * lax.broadcasted_iota(jnp.int32, (16, 2, 128), 0) + lax.broadcasted_iota(jnp.int32, (16, 2, 128), 1)
+    pg, pb, vw = pg_ref[...], pb_ref[...], vw_ref[...]
+
+    def scan(i, state):
+        m = means[i]
+        gate = jax.nn.sigmoid(m * pg + pb)
+        source = (1.0 - gate) * m
+        for k in (0, 1):
+            new = gate[k : k + 1] * state + source[k : k + 1]
+            state = jnp.where(2 * i + k < length, new, state)
+            states[i, k : k + 1, :] = state
+        return state
+
+    lax.fori_loop(0, 16, scan, jnp.zeros((1, D), F32))
+    total = jnp.sum(states[...] * vw.reshape(1, 1, D), axis=-1, keepdims=True)
+    values = jnp.where(frame < length, jnp.broadcast_to(total, (16, 2, 128)), 0.0)
+    vals[0] = values
+    send(vals.at[0], vals.at[1], v_sem.at[0], v_sem.at[1], {"dp": 1 - c})
+
+    wait_final(1)
+
+    def output(i, carry):
+        at = pl.ds(al(i * 16, 16), 16)
+        total = own[at, :] + fin[1, 0, at, :].astype(F32) + fin[1, 1, at, :].astype(F32)
+        hid_ref[at, :] = (after[at, :].astype(F32) + total).astype(BF16)
+        return carry
+
+    lax.fori_loop(0, 8, output, 0)
+
+    arrive(vals.at[1], v_sem.at[1])
+
+    def gaps(v, n):
+        valid = frame < n
+        reward = jnp.sum(jnp.where(frame == n - 1, v, 0.0), axis=(0, 1), keepdims=True)
+        return valid, jnp.where(valid, reward - v, 0.0)
+
+    other = vf_ref[1 - c]
+    count = (length + other).astype(F32)
+    valid, gap = gaps(values, length)
+    valid_o, gap_o = gaps(vals[1], other)
+    add = lambda a: jnp.sum(a, axis=(0, 1), keepdims=True)
+    mean = (add(gap) + add(gap_o)) / count
+    centered = jnp.where(valid, gap - mean, 0.0)
+    centered_o = jnp.where(valid_o, gap_o - mean, 0.0)
+    variance = (add(centered * centered) + add(centered_o * centered_o)) / count
+    adv = jnp.where(valid, centered * lax.rsqrt(variance + 1e-5), 0.0)
+    lane = lax.broadcasted_iota(jnp.int32, (1, 128), 1)
+
+    def own_pair(a):
+        first = jnp.sum(jnp.where(frame == 2 * s, a, 0.0), axis=(0, 1))
+        second = jnp.sum(jnp.where(frame == 2 * s + 1, a, 0.0), axis=(0, 1))
+        return jnp.where(lane == 0, first.reshape(1, 128), second.reshape(1, 128))[:, 0:2]
+
+    fv_ref[...] = own_pair(values)
+    adv_ref[...] = own_pair(adv)
+    for copy in sends:
+        copy.wait_send()
+
+
+def rest(heads, tokens, w_out, mlp_gain, w_up, w_down, pool_gain, pool_bias, value_weight, lengths):
+    vmem = pltpu.VMEM
+    dma = pltpu.SemaphoreType.DMA
+    inside = pl.BlockSpec(memory_space=pltpu.VMEM)
+    outside = pl.BlockSpec(memory_space=pl.ANY)
+    return pl.pallas_call(
+        mlp_kernel,
+        out_shape=(
+            jax.ShapeDtypeStruct((ROWS, D), BF16),
+            jax.ShapeDtypeStruct((1, 2), F32),
+            jax.ShapeDtypeStruct((1, 2), F32),
+        ),
+        in_specs=[pl.BlockSpec(memory_space=pltpu.SMEM)] + [inside] * 6 + [outside] * 3,
+        out_specs=(inside,) * 3,
+        scratch_shapes=[
+            vmem((BLOCK, D), BF16),
+            vmem((D, D), BF16),
+            vmem((D, D), BF16),
+            vmem((2, 4, ROWS, D), BF16),
+            vmem((2, 2, 64, D), BF16),
+            vmem((2, 2, ROWS, D), BF16),
+            vmem((4, ROWS, D), BF16),
+            vmem((ROWS, D), BF16),
+            vmem((ROWS, D), F32),
+            vmem((2 * ROWS, D), BF16),
+            vmem((2, 8, D), F32),
+            vmem((4, 2, D), F32),
+            vmem((16, 2, D), F32),
+            vmem((16, 2, D), F32),
+            vmem((2, 16, 2, 128), F32),
+            dma((3,)),
+            dma((2, 6)),
+            dma((2, 2)),
+            dma((2, 2, 2)),
+            dma((2, 3)),
+            dma((2, 3)),
+            dma((3,)),
+            dma((4,)),
+            dma((15,)),
+            dma((16,)),
+            dma((2,)),
+        ],
+        compiler_params=pltpu.CompilerParams(
+            collective_id=1, has_side_effects=True, vmem_limit_bytes=56 * 2**20
+        ),
+        cost_estimate=pl.CostEstimate(flops=2 * 10**10, bytes_accessed=4 * 10**7, transcendentals=10**6),
+    )(
+        lengths, heads, tokens, mlp_gain.reshape(1, D), pool_gain.reshape(1, D), pool_bias.reshape(1, D),
+        value_weight.reshape(1, D), w_out, w_up, w_down,
+    )
 
 
 def local(
-    tokens,
-    attn_gain,
-    w_qkv,
-    w_out,
-    mlp_gain,
-    w_up,
-    w_down,
-    pool_gain,
-    pool_bias,
-    value_weight,
-    valid_frames,
+    tokens, attn_gain, w_qkv, w_out, mlp_gain, w_up, w_down, pool_gain, pool_bias, value_weight, valid_frames
 ):
-    rows = tokens[0]
-    row_count = rows.shape[0]
-    seq_index = lax.axis_index("seq")
-    tensor_index = lax.axis_index("tensor")
-    roll_index = lax.axis_index("dp")
-    length = valid_frames[roll_index]
-    heads = attention(rows, attn_gain, w_qkv, valid_frames)
-    mixed = heads.transpose(1, 0, 2).reshape(BLOCK, 4 * HEAD_DIM)
-    attn_sum = summed_on_arrival(
-        jnp.dot(mixed, w_out, preferred_element_type=jnp.float32).astype(jnp.bfloat16), "tensor", 0
+    heads = attention(tokens[0], attn_gain, w_qkv, valid_frames)
+    hidden, values, advantages = rest(
+        heads, tokens[0], w_out, mlp_gain, w_up, w_down, pool_gain, pool_bias, value_weight, valid_frames
     )
-    after_attn = (rows.astype(jnp.float32) + attn_sum).astype(jnp.bfloat16)
-    normed2 = rms_norm(after_attn, mlp_gain)
-    up = jax.nn.gelu(
-        jnp.dot(gathered_copies(normed2, "tensor", 0), w_up, preferred_element_type=jnp.float32),
-        approximate=True,
-    ).astype(jnp.bfloat16)
-    down_sum = summed_on_arrival(
-        jnp.dot(up, w_down, preferred_element_type=jnp.float32).astype(jnp.bfloat16), "tensor", 0
-    )
-    hidden = (after_attn.astype(jnp.float32) + down_sum).astype(jnp.bfloat16)
-    local_frame = (tensor_index * row_count + jnp.arange(row_count, dtype=jnp.int32)) // TOK_FRAME
-    selector = (local_frame[None, :] == jnp.arange(FR_DEV, dtype=jnp.int32)[:, None]).astype(
-        jnp.bfloat16
-    )
-    sums = jnp.dot(selector, hidden, preferred_element_type=jnp.float32)
-    sums = over_copies(sums, "tensor")
-    gain, offset, head_weight = (pool_gain, pool_bias, value_weight)
-    means = sums / TOK_FRAME
-    frame_global = seq_index * FR_DEV + jnp.arange(FR_DEV, dtype=jnp.int32)
-    valid = frame_global < length
-    gate = jax.nn.sigmoid(means * gain + offset)
-    decay = jnp.where(valid[:, None], gate, 1.0)
-    source = jnp.where(valid[:, None], (1.0 - gate) * means, 0.0)
-    agg_decay = jnp.ones_like(means[0])
-    agg_source = jnp.zeros_like(means[0])
-    for frame in range(FR_DEV):
-        agg_decay, agg_source = compose((agg_decay, agg_source), (decay[frame], source[frame]))
-    entering = entering_2(
-        (agg_decay, agg_source),
-        "seq",
-        compose,
-        (jnp.ones_like(agg_decay), jnp.zeros_like(agg_source)),
-    )
-    state = entering[1]
-    collected = []
-    for frame in range(FR_DEV):
-        state = decay[frame] * state + source[frame]
-        collected.append(jnp.sum(state * head_weight))
-    partial_values = jnp.stack(collected)
-    values = jnp.where(valid, partial_values, 0.0)
-    pick = jnp.sum(jnp.where(frame_global == length - 1, values, 0.0))
-    count = jnp.sum(valid_frames).astype(jnp.float32)
-    slot = (jnp.arange(lax.axis_size("dp"), dtype=jnp.int32) == roll_index).astype(jnp.float32)
-    entries = jnp.stack([pick, jnp.sum(values), jnp.sum(values * values)])
-    table = over_copies(entries[:, None] * slot[None, :], ("dp", "seq"))
-    finals, first_sums, second_sums = (table[0], table[1], table[2])
-    lengths = valid_frames.astype(jnp.float32)
-    mean = jnp.sum(lengths * finals - first_sums) / count
-    squares = jnp.sum(lengths * finals * finals - 2.0 * finals * first_sums + second_sums) / count
-    variance = squares - mean * mean
-    final = jnp.sum(finals * slot)
-    gap = jnp.where(valid, final - values, 0.0)
-    centered = jnp.where(valid, gap - mean, 0.0)
-    advantages = jnp.where(valid, centered * lax.rsqrt(variance + 1e-05), 0.0)
-    return (hidden[None], values[None], advantages[None])
+    return hidden[None], values, advantages
 
 
 def solution(mesh):

time: 252 us -> 163 us (0.65)
  Pallas kernels: 81.2 us -> 154 us
  starting transfers between devices: 50.8 us -> 0 us
  blocking collectives: 43.2 us -> 0 us
  waiting for transfers between devices: 30.3 us -> 0 us
  matrix products: 18.1 us -> 0 us
  other arithmetic: 16.4 us -> 0 us
  between operations: 3.6 us -> 0.67 us
    pallas_call x0 -> x1, Pallas kernels: none -> 72.7 us  [rest(): pl.pallas_call(mlp_kernel, out_shape=(jax.ShapeDtypeStruct((ROWS, D), BF1...]
    all_to_all x4 -> x0, starting transfers between devices: 50.8 us -> none  [the longest x3 46.2 us: sent_to_all(): return lax.all_to_all(copies, axis, split_axis=0, concat_axis=0, tiled=True)]
    all_to_all x2 -> x0, blocking collectives: 43.2 us -> none  [the longest x1 21.7 us: summed_on_arrival(): blocks = lax.all_to_all(cut_along(array, dim, size), axis, 0, 0, tiled=True)]
    all_to_all x4 -> x0, waiting for transfers between devices: 30.3 us -> none  [the longest x1 16.5 us: summed_on_arrival(): blocks = lax.all_to_all(cut_along(array, dim, size), axis, 0, 0, tiled=True)]
    dot_general x3 -> x0, matrix products: 18.1 us -> none  [the longest x1 16.6 us: local(): jnp.dot(up, w_down, preferred_element_type=jnp.float32).astype(jnp.bfloat16)]
    reduce_sum x9 -> x0, other arithmetic: 7.38 us -> none  [the longest x1 2.57 us: local(): pick = jnp.sum(jnp.where(frame_global == length - 1, values, 0.0))]
    unnamed x24 -> x11, local copies, waits for them, and re-layouts: 3.56 us -> 7.4 us
    select_n x5 -> x0, other arithmetic: 3.44 us -> none  [the longest x1 3.17 us: local(): advantages = jnp.where(valid, centered * lax.rsqrt(variance + 1e-05), 0.0)]
  transfers between devices with their start and end apart: 4 -> 0, of which waited for: 4 -> 0; matrix products, arithmetic and copies ran while one was open for 2% -> 0% of each run, Pallas kernels for 0% -> 0%
where the time goes in v2:
time: 163 us; the launch traced here: 162 us
  Pallas kernels  154 us (94%)
  local copies, waits for them, and re-layouts  7.4 us (5%)
    pallas_call x1, Pallas kernels, attention(): pl.pallas_call(attn_kernel, out_shape=jax.ShapeDtypeStruct((4, BLOCK, HEA...  80.9 us
    pallas_call x1, Pallas kernels, rest(): pl.pallas_call(mlp_kernel, out_shape=(jax.ShapeDtypeStruct((ROWS, D), BF1...  72.7 us
    unnamed x11, local copies, waits for them, and re-layouts  7.4 us

profile of v2, /device:TPU:1, one launch (start us, length us, event | category | flops | bytes accessed | tf_op | source)
XLA Modules:
  0.0 161.6 jit_solution(11244396406187300433)
XLA Ops:
  0.6 0.0 copy-start
  0.6 1.0 copy-done
  1.7 0.0 copy-start.1
  1.7 0.7 copy-done.1
  2.4 0.0 copy-start.2
  2.4 0.7 copy-done.2
  3.0 80.9 %shard_map.130.mixed_ref = bf16[4,512,128]{2,1,0:T(8,128)(2,1)S(1)} custom-call(s32[2]{0:T(128)S(1)} %copy-done.2, bf16[128,2048]{1,0:T(8,128)(2,1)S(1)} %bitcast.8, f32[1,2048]{1,0:T(1,128)S(1)} %bitcast.9, bf16[3,2048,512]{2,1,0:T(8,128)(2,1)} %w_hbm.1), custom_call_target="tpu_custom_call" | custom-call | flops 20000000000 | bytes 20000000 | tf_op jit(solution)/shard_map/pallas_call | solution.py:351
  83.9 0.0 copy-start.3
  83.9 0.8 copy-done.3
  84.7 72.7 %shard_map.131 = (bf16[128,2048]{1,0:T(8,128)(2,1)}, f32[1,2]{1,0:T(1,128)}, f32[1,2]{1,0:T(1,128)}) custom-call(s32[2]{0:T(128)} %vf_ref.3, bf16[4,512,128]{2,1,0:T(8,128)(2,1)} %copy-done.3, bf16[128,2048]{1,0:T(8,128)(2,1)} %bitcast.7, f32[1,2048]{1,0:T(1,128)} %bitcast.11, f32[1,2048]{1,0:T(1,128)} %bitcast.12, f32[1,2048]{1,0:T(1,128)} %bitcast.13, ...), custom_call_target="tpu_custom_call" | custom-call | flops 20000000000 | bytes 40000000 | tf_op jit(solution)/shard_map/pallas_call | solution.py:637
  157.4 1.9 %copy.17 = bf16[1,128,2048]{2,1,0:T(8,128)(2,1)} copy(bf16[1,128,2048]{2,1,0:T(8,128)(2,1)} %bitcast.10) | data formatting | bytes 1048576
  159.2 1.2 copy.18
  160.4 1.2 copy.19
Async XLA Ops:
  0.6 1.0 copy-start
  1.7 0.7 copy-start.1
  2.4 0.7 copy-start.2
  83.9 0.8 copy-start.3

commit v3 on v2

--- a/solution.py
+++ b/solution.py
@@ -11,13 +11,16 @@
 HEAD_DIM = 128
 TOK_FRAME = 256
 ROWS = 128
+HALF = 64
 BLOCK = 512
 D = 2048
+DEPTH = 144
 BF16 = jnp.bfloat16
 F32 = jnp.float32
 MESH = pl.DeviceIdType.MESH
 QSCALE = math.log2(math.e) / math.sqrt(HEAD_DIM)
 NEG = -1e30
+ONWARD = (0, 1)
 
 
 def remote(src, dst, send_sem, recv_sem, where):
@@ -59,14 +62,14 @@
         dst[at, :] = (x * lax.rsqrt(square + 1e-5) * gain_ref[...]).astype(BF16)
         return carry
 
-    lax.fori_loop(0, rows // 16, body, 0)
+    lax.fori_loop(0, rows // 16, body, 0, unroll=True)
 
 
 def attn_kernel(
-    vf_ref, tok_hbm, gain_ref, w_hbm, mixed_ref,
-    tok, w, normed, stage, qx, kx, vx, m_s, acc, o_stage,
-    tl_sem, w_sem, ts_sem, tr_sem, a_send, q_recv, k_recv, v_recv, qs_recv,
-    g_send, gk_recv, gv_recv, r_recv, o_send, o_recv,
+    vf_ref, tok_hbm, gain_hbm, w_hbm, mixed_ref,
+    tok, w, gain_ref, normed, stage, qx, kx, vt, m_s, acc, s0, s1, o_stage,
+    tl_sem, w_sem, ts_sem, tr_sem, a_send, q_recv, k_recv, qs_recv,
+    g_send, gk_recv, r_recv, o_send, o_recv,
 ):
     me = Place()
     c, z, p, g = me.c, me.z, me.p, me.g
@@ -74,8 +77,10 @@
     gp, gm, g2 = (g + 1) % 4, (g + 3) % 4, (g + 2) % 4
     flip = me.flip(p)
 
-    own_in = pltpu.make_async_copy(tok_hbm, tok.at[z], tl_sem)
+    own_in = pltpu.make_async_copy(tok_hbm, tok.at[z], tl_sem.at[0])
     own_in.start()
+    gain_in = pltpu.make_async_copy(gain_hbm, gain_ref, tl_sem.at[1])
+    gain_in.start()
     w_in = [pltpu.make_async_copy(w_hbm.at[k], w.at[k], w_sem.at[k]) for k in range(3)]
     for copy in w_in:
         copy.start()
@@ -92,33 +97,39 @@
     own_in.wait()
     pl.semaphore_wait(barrier, 11)
 
-    lo, hi = pl.ds(0, 64), pl.ds(64, 64)
-    halves = (lo, hi)
+    halves = (pl.ds(0, HALF), pl.ds(HALF, HALF))
     sends = []
 
-    def tok_send(direction, k, t, half):
-        to = zp if direction == 0 else zm
-        copy = remote(
-            tok.at[t, halves[half], :], tok.at[t, halves[half], :],
-            ts_sem.at[direction, k], tr_sem.at[direction, k], {"tensor": to},
-        )
+    def send(src, dst, send_sem, recv_sem, to):
+        copy = remote(src, dst, send_sem, recv_sem, to)
         copy.start()
         sends.append(copy)
 
+    def arrive(ref, sem):
+        remote(ref, ref, sem, sem, {"tensor": zp}).wait_recv()
+
+    def tok_send(direction, k, t, half):
+        ref = tok.at[t, halves[half], :]
+        send(ref, ref, ts_sem.at[direction, k], tr_sem.at[direction, k], {"tensor": zp if direction == 0 else zm})
+
     def tok_wait(direction, k, t, half):
-        remote(
-            tok.at[t, halves[half], :], tok.at[t, halves[half], :],
-            ts_sem.at[direction, k], tr_sem.at[direction, k], {"tensor": zp},
-        ).wait_recv()
+        arrive(tok.at[t, halves[half], :], tr_sem.at[direction, k])
 
     tok_send(0, 0, z, 0)
     tok_send(1, 0, z, 1)
     tok_send(0, 1, z, 1)
     tok_send(1, 1, z, 0)
 
-    def project(t):
-        norm_rows(tok.at[t], gain_ref, normed, ROWS)
-        for k in range(3):
+    stages = (((z, 0), (z, 1)), ((zm, 0), (zp, 1)), ((zm, 1), (zp, 0)), ((z2, 0), (z2, 1)))
+
+    def rows_of(piece):
+        t, half = piece
+        return pl.ds(al(t * ROWS + half * HALF, HALF), HALF)
+
+    def project(n):
+        for k, (t, half) in enumerate(stages[n]):
+            norm_rows(tok.at[t, halves[half], :], gain_ref, normed.at[halves[k], :], HALF)
+        for k in (1, 2, 0):
             for pair in range(2):
                 out = jnp.dot(
                     normed[...], w[k, :, pair * 256 : pair * 256 + 256], preferred_element_type=F32
@@ -126,81 +137,74 @@
                 if k == 0:
                     out = out * QSCALE
                 out = out.astype(BF16)
-                stage[t, 2 * pair, k] = out[:, :128]
-                stage[t, 2 * pair + 1, k] = out[:, 128:]
-
-    def hand_out(t):
-        rows = pl.ds(al(t * ROWS, ROWS), ROWS)
-        for d in (1, 2, 3):
-            h = (p + d) % 4
-            to_q = {"seq": me.seq(h, me.gq(p, g))}
-            to_kv = {"seq": me.seq(h, g)}
-            for k, (dst, sem, to) in enumerate(
-                (
-                    (qx.at[p, rows, pl.ds(0, 128)], q_recv.at[t], to_q),
-                    (kx.at[g * 4 + p, rows, pl.ds(0, 128)], k_recv.at[t], to_kv),
-                    (vx.at[g * 4 + p, rows, pl.ds(0, 128)], v_recv.at[t], to_kv),
-                )
-            ):
-                copy = remote(stage.at[t, h, k], dst, a_send.at[t, d - 1, k], sem, to)
-                copy.start()
-                sends.append(copy)
-        kx[g * 4 + p, rows, 0:128] = stage[t, p, 1]
-        vx[g * 4 + p, rows, 0:128] = stage[t, p, 2]
+                at = slice((2 - k) * 128, (3 - k) * 128)
+                stage[n, 2 * pair, :, at] = out[:, :128]
+                stage[n, 2 * pair + 1, :, at] = out[:, 128:]
+
+    both = pl.ds(0, 256)
+    third = pl.ds(256, 128)
+    lanes = pl.ds(0, HEAD_DIM)
+
+    def pieces(n):
+        if n in (0, 3):
+            return ((pl.ds(0, ROWS), pl.ds(al(stages[n][0][0] * ROWS, ROWS), ROWS)),)
+        return tuple((halves[k], rows_of(piece)) for k, piece in enumerate(stages[n]))
+
+    def hand_out(n):
+        for k, (buf, sem, part) in enumerate(((kx, k_recv, both), (qx, q_recv, third))):
+            for d in (2, 1, 3):
+                h = (p + d) % 4
+                to = {"seq": me.seq(h, me.gq(p, g) if k else g)}
+                slot = p if k else g * 4 + p
+                for half, (src, dst) in enumerate(pieces(n)):
+                    send(
+                        stage.at[n, h, src, part], buf.at[slot, dst, lanes if k else both],
+                        a_send.at[n, d - 1, k, half], sem.at[n], to,
+                    )
+        for src, dst in pieces(n):
+            kx[g * 4 + p, dst, 0:256] = stage[n, p, src, 0:256]
 
         @pl.when(flip == 1)
         def _():
-            remote(
-                stage.at[t, p, 0], qx.at[p, rows, pl.ds(0, 128)], a_send.at[t, 3, 0], qs_recv.at[t],
-                {"seq": me.seq(p, 3 - g)},
-            ).start()
+            for half, (src, dst) in enumerate(pieces(n)):
+                remote(
+                    stage.at[n, p, src, third], qx.at[p, dst, lanes],
+                    a_send.at[n, 3, 0, half], qs_recv.at[n], {"seq": me.seq(p, 3 - g)},
+                ).start()
 
         @pl.when(flip == 0)
         def _():
-            qx[p, rows, 0:128] = stage[t, p, 0]
-
-    three = pl.ds(0, 3)
-
-    def three_in(sem, buf, t):
-        rows = pl.ds(al(t * ROWS, ROWS), ROWS)
-        ref = buf.at[three, rows, pl.ds(0, 128)]
-        remote(ref, ref, sem, sem, {"tensor": zp}).wait_recv()
-
-    def group_ref(buf, gg, t):
-        return buf.at[pl.ds(gg * 4, 4), pl.ds(al(t * ROWS, ROWS), ROWS), pl.ds(0, 128)]
-
-    def ring_out(t):
-        three_in(k_recv.at[t], kx, t)
-        three_in(v_recv.at[t], vx, t)
+            for src, dst in pieces(n):
+                qx[p, dst, 0:128] = stage[n, p, src, 256:384]
+
+    def stage_in(count, buf, sem):
+        arrive(buf.at[pl.ds(0, count), pl.ds(0, ROWS), lanes if buf is qx else both], sem)
+
+    def ring_out(n):
+        stage_in(3, kx, k_recv.at[n])
         for direction in (0, 1):
             to = {"seq": me.seq(p, gp if direction == 0 else gm)}
-            pair = ((kx, gk_recv, 0), (vx, gv_recv, 1))
-            for buf, sem, k in pair if direction == 0 else pair[::-1]:
-                ref = group_ref(buf, g, t)
-                copy = remote(ref, ref, g_send.at[direction, t, k], sem.at[direction, t], to)
-                copy.start()
-                sends.append(copy)
-
-    def ring_wait(buf, sem, gg, t):
-        ref = group_ref(buf, gg, t)
-        remote(ref, ref, sem, sem, {"tensor": zp}).wait_recv()
-
-    def relay(t):
-        ring_wait(kx, gk_recv.at[0, t], gm, t)
-        ref = group_ref(kx, gm, t)
-        copy = remote(ref, ref, g_send.at[0, t, 2], r_recv.at[0, t], {"seq": me.seq(p, gp)})
-        copy.start()
-        sends.append(copy)
-        ring_wait(vx, gv_recv.at[1, t], gp, t)
-        ref = group_ref(vx, gp, t)
-        copy = remote(ref, ref, g_send.at[1, t, 2], r_recv.at[1, t], {"seq": me.seq(p, gm)})
-        copy.start()
-        sends.append(copy)
-
+            for half, (_, dst) in enumerate(pieces(n)):
+                ref = kx.at[pl.ds(g * 4, 4), dst, both]
+                send(ref, ref, g_send.at[direction, n, half], gk_recv.at[direction, n], to)
+
+    def relay(n):
+        for direction in sorted(set(ONWARD)):
+            stage_in(4, kx, gk_recv.at[direction, n])
+            source, to = (gm, gp) if direction == 0 else (gp, gm)
+            if ONWARD[0] == ONWARD[1]:
+                runs = pieces(n)
+            else:
+                runs = ((0, rows_of(stages[n][direction])),)
+            for half, (_, dst) in enumerate(runs):
+                ref = kx.at[pl.ds(source * 4, 4), dst, both]
+                send(ref, ref, g_send.at[direction, n, 2 + half], r_recv.at[n], {"seq": me.seq(p, to)})
+
+    gain_in.wait()
     for copy in w_in:
         copy.wait()
-    project(z)
-    hand_out(z)
+    project(0)
+    hand_out(0)
 
     length = vf_ref[c]
     lane = lax.broadcasted_iota(jnp.int32, (BLOCK, 128), 1)
@@ -216,130 +220,141 @@
                 me.seq(i, me.gq(i, g)) == block
             ).astype(jnp.int32)
         bias = jnp.where((mine > 0) & (row >= TOK_FRAME), NEG, bias)
-        kx[slot, :, 128:256] = bias.astype(BF16)
-        vx[slot, :, 128:256] = jnp.ones((BLOCK, 128), BF16)
+        kx[slot, :, 256:384] = bias.astype(BF16)
+        vt[slot, 128:DEPTH, :] = jnp.ones((DEPTH - 128, BLOCK), BF16)
         return carry
 
     lax.fori_loop(0, 16, fill, 0)
+    kx[16, :, 0:256] = jnp.zeros((BLOCK, 256), BF16)
+    kx[16, :, 256:384] = jnp.where(lane == 0, NEG, 0.0).astype(BF16)
+    vt[16] = jnp.zeros((DEPTH, BLOCK), BF16)
     for i in range(4):
         on = (lane == 0) | ((lane == 1 + i) & (row < TOK_FRAME))
         qx[i, :, 128:256] = jnp.where(on, 1.0, 0.0).astype(BF16)
-        m_s[i] = jnp.full((BLOCK, 128), -1e38, F32)
-        acc[i] = jnp.zeros((BLOCK, 256), F32)
+        m_s[i] = jnp.full((8, BLOCK), -1e38, F32)
+        acc[i] = jnp.zeros((DEPTH, BLOCK), F32)
 
     tok_wait(0, 0, zm, 0)
     tok_send(0, 2, zm, 0)
     tok_wait(1, 0, zp, 1)
     tok_send(1, 2, zp, 1)
-    ring_out(z)
+    ring_out(0)
+    project(1)
+    hand_out(1)
     tok_wait(0, 1, zm, 1)
-    project(zm)
-    hand_out(zm)
     tok_wait(1, 1, zp, 0)
-    project(zp)
-    hand_out(zp)
-    relay(z)
-    ring_out(zm)
-    ring_out(zp)
+    project(2)
+    hand_out(2)
+    ring_out(1)
+    relay(0)
     tok_wait(0, 2, z2, 0)
     tok_wait(1, 2, z2, 1)
-    project(z2)
-    hand_out(z2)
-    relay(zm)
-    relay(zp)
-    ring_out(z2)
-    for k in range(4):
-        t = (z + k) % 4
-        three_in(q_recv.at[t], qx, t)
+    project(3)
+    hand_out(3)
+    ring_out(2)
+    relay(1)
+    ring_out(3)
+    relay(2)
+    for n in range(4):
+        stage_in(3, qx, q_recv.at[n])
 
         @pl.when(flip == 1)
         def _():
-            ref = qx.at[p, pl.ds(al(t * ROWS, ROWS), ROWS), pl.ds(0, 128)]
-            remote(ref, ref, qs_recv.at[t], qs_recv.at[t], {"tensor": zp}).wait_recv()
-
-    def group(gg):
-        def per_q(i, carry):
-            n = me.seq(i, me.gq(i, g))
-            first = me.seq(0, gg)
-            step = 4 * (1 - c) + c
-            count = jnp.clip((n - first + step) // step, 0, 4)
-
-            def pair(j, carry):
-                slot = gg * 4 + j
-                for a in range(2):
-                    at = pl.ds(a * 256, 256)
-                    s = lax.dot_general(
-                        qx[i, at, :], kx[slot], (((1,), (1,)), ((), ())), preferred_element_type=F32
-                    )
-                    before = m_s[i, at, :]
-                    after = jnp.maximum(before, jnp.max(s, axis=1, keepdims=True))
-                    weights = jnp.exp2(s - after[:, :1]).astype(BF16)
-                    keep = jnp.exp2(before - after)
-                    m_s[i, at, :] = after
-                    acc[i, at, :] = acc[i, at, :] * jnp.concatenate([keep, keep], axis=1) + jnp.dot(
-                        weights, vx[slot], preferred_element_type=F32
-                    )
-                return carry
-
-            lax.fori_loop(0, count, pair, 0)
+            stage_in(1, qx, qs_recv.at[n])
+
+    def turn(gg):
+        def body(j, carry):
+            vt[gg * 4 + j, 0:128, :] = kx[gg * 4 + j, :, 0:128].T
             return carry
 
-        lax.fori_loop(0, 4, per_q, 0)
-
-    group(g)
-    relay(z2)
-    for k in range(4):
-        ring_wait(vx, gv_recv.at[0, (z + k) % 4], gm, (z + k) % 4)
-    group(gm)
-    for k in range(4):
-        ring_wait(kx, gk_recv.at[1, (z + k) % 4], gp, (z + k) % 4)
-    group(gp)
-    for k in range(4):
-        ring_wait(kx, r_recv.at[0, (z + k) % 4], g2, (z + k) % 4)
-        ring_wait(vx, r_recv.at[1, (z + k) % 4], g2, (z + k) % 4)
-    group(g2)
-
-    def finish(i):
-        o_stage[i] = (acc[i, :, 0:128] / acc[i, :, 128:256]).astype(BF16)
+        lax.fori_loop(0, 4, body, 0)
+
+    turn(g)
+    relay(3)
+    for direction in (0, 1):
+        if direction not in ONWARD:
+            for n in range(4):
+                stage_in(4, kx, gk_recv.at[direction, n])
+    turn(gm)
+    turn(gp)
+    for n in range(4):
+        stage_in(4, kx, r_recv.at[n])
+    turn(g2)
+
+    def slot_of(b, count):
+        pad = b // count
+        slot = (1 - c) * ((b % 4) * 4 + b // 4) + c * b
+        return (1 - pad) * slot + pad * 16
+
+    def score(i, slot, buf):
+        for a in (0, 256):
+            buf[:, a : a + 256] = lax.dot_general(
+                kx[slot, :, 128:384], qx[i, a : a + 256, :], (((1,), (1,)), ((), ())), preferred_element_type=F32
+            )
+
+    def gather(i, slot, buf):
+        for a in (0, 256):
+            at = slice(a, a + 256)
+            s = buf[:, at]
+            before = m_s[i, 0:1, at]
+            peak = jnp.maximum(before, jnp.max(s, axis=0, keepdims=True))
+            m_s[i, 0:1, at] = peak
+            weights = jnp.exp2(s - peak).astype(BF16)
+            acc[i, :, at] = acc[i, :, at] * jnp.exp2(before - peak) + jnp.dot(
+                vt[slot], weights, preferred_element_type=F32
+            )
+
+    def back(i):
+        return remote(
+            o_stage.at[i], mixed_ref.at[p], o_send.at[i], o_recv.at[p], {"seq": me.seq(i, me.gq(i, g))}
+        )
+
+    score(0, 0, s0)
+    for i in range(4):
+        count = me.seq(i, me.gq(i, g)) + 1
+        steps = (count + 1) // 2
+
+        def two(n, carry):
+            score(i, slot_of(2 * n + 1, count), s1)
+            gather(i, slot_of(2 * n, count), s0)
+            over = (n + 1) // steps
+            score(min(i + 1, 3) * over + i * (1 - over), (1 - over) * slot_of(2 * n + 2, count), s0)
+            gather(i, slot_of(2 * n + 1, count), s1)
+            return carry
+
+        lax.fori_loop(0, steps, two, 0)
+        out = acc[i, 0:128, :] / acc[i, 128:129, :]
+        o_stage[i] = out.T.astype(BF16)
+        stays = (1 - flip) * (p == i).astype(jnp.int32)
+
+        @pl.when(stays == 0)
+        def _():
+            back(i).start()
+
+        @pl.when(stays == 1)
+        def _():
+            mixed_ref[p] = o_stage[i]
 
     for d in (1, 2, 3):
-        i = (p + d) % 4
-        finish(i)
-        copy = remote(
-            o_stage.at[i], mixed_ref.at[p], o_send.at[d - 1], o_recv.at[p],
-            {"seq": me.seq(i, me.gq(i, g))},
-        )
-        copy.start()
-        sends.append(copy)
-    finish(p)
+        h = (p + d) % 4
+        arrive(mixed_ref.at[h], o_recv.at[h])
 
     @pl.when(flip == 1)
     def _():
-        remote(
-            o_stage.at[p], mixed_ref.at[p], o_send.at[3], o_recv.at[p], {"seq": me.seq(p, 3 - g)}
-        ).start()
-
-    @pl.when(flip == 0)
-    def _():
-        mixed_ref[p] = o_stage[p]
-
-    for d in (1, 2, 3):
-        h = (p + d) % 4
-        remote(o_stage.at[0], mixed_ref.at[h], o_send.at[0], o_recv.at[h], {"tensor": zp}).wait_recv()
-
-    @pl.when(flip == 1)
-    def _():
-        back = remote(
-            o_stage.at[p], mixed_ref.at[p], o_send.at[3], o_recv.at[p], {"seq": me.seq(p, 3 - g)}
-        )
-        back.wait_recv()
-        back.wait_send()
-        for t in range(4):
-            rows = pl.ds(t * ROWS, ROWS)
-            remote(
-                stage.at[t, p, 0], qx.at[p, rows, pl.ds(0, 128)], a_send.at[t, 3, 0], qs_recv.at[t],
-                {"seq": me.seq(p, 3 - g)},
-            ).wait_send()
+        arrive(mixed_ref.at[p], o_recv.at[p])
+        for n in range(4):
+            for half, (src, dst) in enumerate(pieces(n)):
+                remote(
+                    stage.at[n, p, src, third], qx.at[p, dst, lanes],
+                    a_send.at[n, 3, 0, half], qs_recv.at[n], {"seq": me.seq(p, 3 - g)},
+                ).wait_send()
+
+    for i in range(4):
+        stays = (1 - flip) * (p == i).astype(jnp.int32)
+
+        @pl.when(stays == 0)
+        def _():
+            back(i).wait_send()
 
     for copy in sends:
         copy.wait_send()
@@ -348,40 +363,37 @@
 def attention(tokens, gain, w_qkv, lengths):
     vmem = pltpu.VMEM
     dma = pltpu.SemaphoreType.DMA
+    outside = pl.BlockSpec(memory_space=pl.ANY)
     return pl.pallas_call(
         attn_kernel,
         out_shape=jax.ShapeDtypeStruct((4, BLOCK, HEAD_DIM), BF16),
-        in_specs=[
-            pl.BlockSpec(memory_space=pltpu.SMEM),
-            pl.BlockSpec(memory_space=pl.ANY),
-            pl.BlockSpec(memory_space=pltpu.VMEM),
-            pl.BlockSpec(memory_space=pl.ANY),
-        ],
+        in_specs=[pl.BlockSpec(memory_space=pltpu.SMEM), outside, outside, outside],
         out_specs=pl.BlockSpec(memory_space=pltpu.VMEM),
         scratch_shapes=[
             vmem((4, ROWS, D), BF16),
             vmem((3, D, BLOCK), BF16),
+            vmem((1, D), F32),
             vmem((ROWS, D), BF16),
-            vmem((4, 4, 3, ROWS, HEAD_DIM), BF16),
+            vmem((4, 4, ROWS, 384), BF16),
             vmem((4, BLOCK, 256), BF16),
-            vmem((16, BLOCK, 256), BF16),
-            vmem((16, BLOCK, 256), BF16),
-            vmem((4, BLOCK, 128), F32),
-            vmem((4, BLOCK, 256), F32),
+            vmem((17, BLOCK, 384), BF16),
+            vmem((17, DEPTH, BLOCK), BF16),
+            vmem((4, 8, BLOCK), F32),
+            vmem((4, DEPTH, BLOCK), F32),
+            vmem((BLOCK, BLOCK), F32),
+            vmem((BLOCK, BLOCK), F32),
             vmem((4, BLOCK, HEAD_DIM), BF16),
-            dma,
+            dma((2,)),
             dma((3,)),
             dma((2, 3)),
             dma((2, 3)),
-            dma((4, 4, 3)),
+            dma((4, 4, 2, 2)),
             dma((4,)),
             dma((4,)),
             dma((4,)),
+            dma((2, 4, 4)),
+            dma((2, 4)),
             dma((4,)),
-            dma((2, 4, 3)),
-            dma((2, 4)),
-            dma((2, 4)),
-            dma((2, 4)),
             dma((4,)),
             dma((4,)),
         ],

time: 163 us -> 145 us (0.89)
  Pallas kernels: 154 us -> 135 us
    pallas_call x1, Pallas kernels: 80.9 us -> 64 us  [attention(): pl.pallas_call(attn_kernel, out_shape=jax.ShapeDtypeStruct((4, BLOCK, HEA...]
where the time goes in v3:
time: 145 us; the launch traced here: 143 us
  Pallas kernels  135 us (93%)
  local copies, waits for them, and re-layouts  7.4 us (5%)
    pallas_call x1, Pallas kernels, rest(): pl.pallas_call(mlp_kernel, out_shape=(jax.ShapeDtypeStruct((ROWS, D), BF1...  71.2 us
    pallas_call x1, Pallas kernels, attention(): pl.pallas_call(attn_kernel, out_shape=jax.ShapeDtypeStruct((4, BLOCK, HEA...  64 us
    unnamed x11, local copies, waits for them, and re-layouts  7.4 us

profile of v3, /device:TPU:1, one launch (start us, length us, event | category | flops | bytes accessed | tf_op | source)
XLA Modules:
  0.0 143.3 jit_solution(6833001949627989211)
XLA Ops:
  0.6 0.0 copy-start
  0.6 1.0 copy-done
  1.7 0.0 copy-start.1
  1.7 0.7 copy-done.1
  2.4 0.0 copy-start.2
  2.4 0.7 copy-done.2
  3.0 64.0 %shard_map.130.mixed_ref = bf16[4,512,128]{2,1,0:T(8,128)(2,1)S(1)} custom-call(s32[2]{0:T(128)S(1)} %copy-done.2, bf16[128,2048]{1,0:T(8,128)(2,1)S(1)} %bitcast.8, f32[1,2048]{1,0:T(1,128)S(1)} %bitcast.9, bf16[3,2048,512]{2,1,0:T(8,128)(2,1)} %w_hbm.1), custom_call_target="tpu_custom_call" | custom-call | flops 20000000000 | bytes 20000000 | tf_op jit(solution)/shard_map/pallas_call | solution.py:367
  67.0 0.0 copy-start.3
  67.0 0.8 copy-done.3
  67.8 71.2 %shard_map.131 = (bf16[128,2048]{1,0:T(8,128)(2,1)}, f32[1,2]{1,0:T(1,128)}, f32[1,2]{1,0:T(1,128)}) custom-call(s32[2]{0:T(128)} %vf_ref.3, bf16[4,512,128]{2,1,0:T(8,128)(2,1)} %copy-done.3, bf16[128,2048]{1,0:T(8,128)(2,1)} %bitcast.7, f32[1,2048]{1,0:T(1,128)} %bitcast.11, f32[1,2048]{1,0:T(1,128)} %bitcast.12, f32[1,2048]{1,0:T(1,128)} %bitcast.13, ...), custom_call_target="tpu_custom_call" | custom-call | flops 20000000000 | bytes 40000000 | tf_op jit(solution)/shard_map/pallas_call | solution.py:649
  139.1 1.9 %copy.17 = bf16[1,128,2048]{2,1,0:T(8,128)(2,1)} copy(bf16[1,128,2048]{2,1,0:T(8,128)(2,1)} %bitcast.10) | data formatting | bytes 1048576
  140.9 1.2 copy.18
  142.1 1.2 copy.19
Async XLA Ops:
  0.6 1.0 copy-start
  1.7 0.7 copy-start.1
  2.4 0.7 copy-start.2
  67.0 0.8 copy-start.3

commit v4 on v3

v4 whole, which is shorter than its diff:
```python
import functools
import math

import jax
import jax.numpy as jnp
from jax import lax
from jax.experimental import pallas as pl
from jax.experimental.pallas import tpu as pltpu
from jax.sharding import PartitionSpec as P

HEAD_DIM = 128
TOK_FRAME = 256
ROWS = 128
HALF = 64
BLOCK = 512
D = 2048
DEPTH = 144
BF16 = jnp.bfloat16
F32 = jnp.float32
MESH = pl.DeviceIdType.MESH
QSCALE = math.log2(math.e) / math.sqrt(HEAD_DIM)
NEG = -1e30
ONWARD = (0, 1)
HOOKS = (9, 11)


def remote(src, dst, send_sem, recv_sem, where):
    return pltpu.make_async_remote_copy(
        src_ref=src, dst_ref=dst, send_sem=send_sem, recv_sem=recv_sem,
        device_id=where, device_id_type=MESH,
    )


def al(i, m):
    return pl.multiple_of(i, m)


class Place:
    def __init__(self):
        self.c = lax.axis_index("dp")
        s = lax.axis_index("seq")
        self.s = s
        self.z = lax.axis_index("tensor")
        y, x = s // 4, s % 4
        self.p = y * (1 - self.c) + x * self.c
        self.g = x * (1 - self.c) + y * self.c

    def seq(self, p, g):
        return (p * 4 + g) * (1 - self.c) + (g * 4 + p) * self.c

    def flip(self, p):
        return (1 - self.c) * (1 - p % 2) + self.c * (p // 2)

    def gq(self, p, g):
        return g + self.flip(p) * (3 - 2 * g)


def norm_rows(src, gain_ref, dst, rows):
    def body(i, carry):
        at = pl.ds(al(i * 16, 16), 16)
        x = src[at, :].astype(F32)
        square = jnp.mean(x * x, axis=-1, keepdims=True)
        dst[at, :] = (x * lax.rsqrt(square + 1e-5) * gain_ref[...]).astype(BF16)
        return carry

    lax.fori_loop(0, rows // 16, body, 0, unroll=True)


def gelu(x):
    return 0.5 * x * (1.0 + jnp.tanh(math.sqrt(2.0 / math.pi) * (x + 0.044715 * (x * x * x))))


def layer_kernel(
    vf_ref, tok_hbm, w_hbm, wo_hbm, wu_hbm, wd_hbm, g1_hbm, g2_hbm, pg_hbm, pb_hbm, vw_hbm,
    hid_ref, fv_ref, adv_ref,
    tok, w, small, normed, stage, qx, kx, vt, m_s, acc, s0, s1, o_stage, mx, wo, wu, wd,
    part, mid, fin, nrm, up, fs, zs, means, states, vals,
    tl_sem, w_sem, ts_sem, tr_sem, a_send, q_recv, k_recv, qs_recv,
    g_send, gk_recv, r_recv, o_send, o_recv, m_send, m_recv, w1_send, w1_recv, w2_send, w2_recv, w2r_recv,
    d_send, d_recv, rs_send, mid_recv, fin_recv, z_send, z_recv, s_send, s_recv, v_sem,
):
    me = Place()
    c, s, z, p, g = me.c, me.s, me.z, me.p, me.g
    zp, zm, z2 = (z + 1) % 4, (z + 3) % 4, (z + 2) % 4
    gp, gm, g2 = (g + 1) % 4, (g + 3) % 4, (g + 2) % 4
    flip = me.flip(p)
    gain_ref, gain2_ref = small.at[0:1, :], small.at[1:2, :]

    own_in = pltpu.make_async_copy(tok_hbm, tok.at[z], tl_sem.at[0])
    own_in.start()
    small_in = [
        pltpu.make_async_copy(src, small.at[k : k + 1, :], tl_sem.at[1 + k])
        for k, src in enumerate((g1_hbm, g2_hbm, pg_hbm, pb_hbm, vw_hbm))
    ]
    small_in[0].start()
    w_in = [pltpu.make_async_copy(w_hbm.at[k], w.at[k], w_sem.at[k]) for k in range(3)]
    for copy in w_in:
        copy.start()
    late_in = [
        pltpu.make_async_copy(wo_hbm, wo.at[pl.ds(al(z * BLOCK, BLOCK), BLOCK), :], w_sem.at[3]),
        pltpu.make_async_copy(wu_hbm, wu, w_sem.at[4]),
        pltpu.make_async_copy(wd_hbm, wd, w_sem.at[5]),
    ]

    barrier = pltpu.get_barrier_semaphore()
    for t in (zp, zm, z2):
        pl.semaphore_signal(barrier, inc=1, device_id={"tensor": t}, device_id_type=MESH)
    for d in range(1, 16):
        pl.semaphore_signal(barrier, inc=1, device_id={"seq": (s + d) % 16}, device_id_type=MESH)
    pl.semaphore_signal(barrier, inc=1, device_id={"dp": 1 - c}, device_id_type=MESH)
    own_in.wait()
    pl.semaphore_wait(barrier, 19)

    halves = (pl.ds(0, HALF), pl.ds(HALF, HALF))
    sends = []

    def send(src, dst, send_sem, recv_sem, to):
        copy = remote(src, dst, send_sem, recv_sem, to)
        copy.start()
        sends.append(copy)

    def start_only(src, dst, send_sem, recv_sem, to):
        remote(src, dst, send_sem, recv_sem, to).start()

    def arrive(ref, sem):
        remote(ref, ref, sem, sem, {"tensor": zp}).wait_recv()

    def tok_send(direction, k, t, half):
        ref = tok.at[t, halves[half], :]
        start_only(ref, ref, ts_sem.at[direction, k], tr_sem.at[direction, k], {"tensor": zp if direction == 0 else zm})

    def tok_wait(direction, k, t, half):
        arrive(tok.at[t, halves[half], :], tr_sem.at[direction, k])

    tok_send(0, 0, z, 0)
    tok_send(1, 0, z, 1)
    tok_send(0, 1, z, 1)
    tok_send(1, 1, z, 0)

    stages = (((z, 0), (z, 1)), ((zm, 0), (zp, 1)), ((zm, 1), (zp, 0)), ((z2, 0), (z2, 1)))

    def rows_of(piece):
        t, half = piece
        return pl.ds(al(t * ROWS + half * HALF, HALF), HALF)

    def project(n):
        for k, (t, half) in enumerate(stages[n]):
            norm_rows(tok.at[t, halves[half], :], gain_ref, normed.at[halves[k], :], HALF)
        for k in (1, 2, 0):
            for pair in range(2):
                out = jnp.dot(
                    normed[...], w[k, :, pair * 256 : pair * 256 + 256], preferred_element_type=F32
                )
                if k == 0:
                    out = out * QSCALE
                out = out.astype(BF16)
                at = slice((2 - k) * 128, (3 - k) * 128)
                stage[n, 2 * pair, :, at] = out[:, :128]
                stage[n, 2 * pair + 1, :, at] = out[:, 128:]

    both = pl.ds(0, 256)
    third = pl.ds(256, 128)
    lanes = pl.ds(0, HEAD_DIM)

    def pieces(n):
        if n in (0, 3):
            return ((pl.ds(0, ROWS), pl.ds(al(stages[n][0][0] * ROWS, ROWS), ROWS)),)
        return tuple((halves[k], rows_of(piece)) for k, piece in enumerate(stages[n]))

    def hand_out(n):
        for k, (buf, sem, part) in enumerate(((kx, k_recv, both), (qx, q_recv, third))):
            for d in (2, 1, 3):
                h = (p + d) % 4
                to = {"seq": me.seq(h, me.gq(p, g) if k else g)}
                slot = p if k else g * 4 + p
                for half, (src, dst) in enumerate(pieces(n)):
                    send(
                        stage.at[n, h, src, part], buf.at[slot, dst, lanes if k else both],
                        a_send.at[n, d - 1, k, half], sem.at[n], to,
                    )
        for src, dst in pieces(n):
            kx[g * 4 + p, dst, 0:256] = stage[n, p, src, 0:256]

        @pl.when(flip == 1)
        def _():
            for half, (src, dst) in enumerate(pieces(n)):
                remote(
                    stage.at[n, p, src, third], qx.at[p, dst, lanes],
                    a_send.at[n, 3, 0, half], qs_recv.at[n], {"seq": me.seq(p, 3 - g)},
                ).start()

        @pl.when(flip == 0)
        def _():
            for src, dst in pieces(n):
                qx[p, dst, 0:128] = stage[n, p, src, 256:384]

    def stage_in(count, buf, sem):
        arrive(buf.at[pl.ds(0, count), pl.ds(0, ROWS), lanes if buf is qx else both], sem)

    def ring_out(n):
        stage_in(3, kx, k_recv.at[n])
        for direction in (0, 1):
            to = {"seq": me.seq(p, gp if direction == 0 else gm)}
            for half, (_, dst) in enumerate(pieces(n)):
                ref = kx.at[pl.ds(g * 4, 4), dst, both]
                send(ref, ref, g_send.at[direction, n, half], gk_recv.at[direction, n], to)

    def relay(n):
        for direction in sorted(set(ONWARD)):
            stage_in(4, kx, gk_recv.at[direction, n])
            source, to = (gm, gp) if direction == 0 else (gp, gm)
            if ONWARD[0] == ONWARD[1]:
                runs = pieces(n)
            else:
                runs = ((0, rows_of(stages[n][direction])),)
            for half, (_, dst) in enumerate(runs):
                ref = kx.at[pl.ds(source * 4, 4), dst, both]
                send(ref, ref, g_send.at[direction, n, 2 + half], r_recv.at[n], {"seq": me.seq(p, to)})

    def wo_rows(t, k, first, count):
        return wo.at[pl.ds(al(t * BLOCK + c * 256 + k * 64 + first, 32), count), :]

    def w1_copy(direction, k):
        to = zp if direction == 0 else zm
        t, first = ((z, 0), (z, 32), (zm, 0))[k] if direction == 0 else ((z, 32), (z, 0), (zp, 32))[k]
        ref = wo_rows(t, g, first, 32)
        return remote(ref, ref, w1_send.at[direction, k], w1_recv.at[direction, k], {"tensor": to})

    def w1_arrive(direction, k):
        arrive(wo.at[pl.ds(0, 32), :], w1_recv.at[direction, k])

    def w2_own():
        copies = []
        for direction in (0, 1):
            to = {"seq": me.seq(p, gp if direction == 0 else gm)}
            for k, t in enumerate((zp, zm, z2)):
                ref = wo_rows(t, g, 0, 64)
                copies.append(remote(ref, ref, w2_send.at[direction, k], w2_recv.at[direction], to))
        return copies

    def w2_relay():
        copies = []
        for direction in (0, 1):
            source, to = (gm, gp) if direction == 0 else (gp, gm)
            for k, ref in enumerate(
                (wo_rows(zm if direction else zp, source, 0, 64), wo_rows(z2, source, 32 * direction, 32))
            ):
                copies.append(
                    remote(ref, ref, w2_send.at[direction, 3 + k], w2r_recv.at[direction], {"seq": me.seq(p, to)})
                )
        return copies

    def d2d(n):
        k = (g, gm, gp, g2)[n]
        return [
            remote(ref, ref, d_send.at[n, i], d_recv, {"dp": 1 - c})
            for i, ref in enumerate(wo_rows(t, k, 0, 64) for t in (zp, zm, z2))
        ]

    def start(copies):
        for copy in copies:
            copy.start()

    small_in[0].wait()
    for copy in w_in:
        copy.wait()
    start(late_in)
    start(small_in[1:])
    project(0)
    hand_out(0)

    length = vf_ref[c]
    lane = lax.broadcasted_iota(jnp.int32, (BLOCK, 128), 1)
    row = lax.broadcasted_iota(jnp.int32, (BLOCK, 128), 0)

    def fill(slot, carry):
        block = me.seq(slot % 4, slot // 4)
        frame = 2 * block + row // TOK_FRAME
        bias = jnp.where((lane == 0) & (frame >= length), NEG, 0.0)
        mine = 0
        for i in range(4):
            mine = mine + (lane == 1 + i).astype(jnp.int32) * (
                me.seq(i, me.gq(i, g)) == block
            ).astype(jnp.int32)
        bias = jnp.where((mine > 0) & (row >= TOK_FRAME), NEG, bias)
        kx[slot, :, 256:384] = bias.astype(BF16)
        vt[slot, 128:DEPTH, :] = jnp.ones((DEPTH - 128, BLOCK), BF16)
        return carry

    lax.fori_loop(0, 16, fill, 0)
    kx[16, :, 0:256] = jnp.zeros((BLOCK, 256), BF16)
    kx[16, :, 256:384] = jnp.where(lane == 0, NEG, 0.0).astype(BF16)
    vt[16] = jnp.zeros((DEPTH, BLOCK), BF16)
    for i in range(4):
        on = (lane == 0) | ((lane == 1 + i) & (row < TOK_FRAME))
        qx[i, :, 128:256] = jnp.where(on, 1.0, 0.0).astype(BF16)

    tok_wait(0, 0, zm, 0)
    tok_send(0, 2, zm, 0)
    tok_wait(1, 0, zp, 1)
    tok_send(1, 2, zp, 1)
    ring_out(0)
    project(1)
    hand_out(1)
    tok_wait(0, 1, zm, 1)
    tok_wait(1, 1, zp, 0)
    project(2)
    hand_out(2)
    ring_out(1)
    relay(0)
    tok_wait(0, 2, z2, 0)
    tok_wait(1, 2, z2, 1)
    project(3)
    hand_out(3)
    late_in[0].wait()
    start([w1_copy(0, 0), w1_copy(1, 0), w1_copy(0, 1), w1_copy(1, 1)])
    ring_out(2)
    relay(1)
    ring_out(3)
    relay(2)
    for n in range(4):
        stage_in(3, qx, q_recv.at[n])

        @pl.when(flip == 1)
        def _():
            stage_in(1, qx, qs_recv.at[n])

    def turn(gg):
        def body(j, carry):
            vt[gg * 4 + j, 0:128, :] = kx[gg * 4 + j, :, 0:128].T
            return carry

        lax.fori_loop(0, 4, body, 0)

    w1_arrive(0, 0)
    w1_copy(0, 2).start()
    w1_arrive(1, 0)
    w1_copy(1, 2).start()
    turn(g)
    relay(3)
    for direction in (0, 1):
        if direction not in ONWARD:
            for n in range(4):
                stage_in(4, kx, gk_recv.at[direction, n])
    turn(gm)
    turn(gp)
    for n in range(4):
        stage_in(4, kx, r_recv.at[n])
    turn(g2)
    for direction in (0, 1):
        for k in (1, 2):
            w1_arrive(direction, k)
    start(w2_own())
    start(d2d(0))

    def slot_of(b, count):
        pad = b // count
        slot = (1 - c) * ((b % 4) * 4 + b // 4) + c * b
        return (1 - pad) * slot + pad * 16

    def score(i, a, slot, buf):
        buf[...] = lax.dot_general(
            kx[slot, :, 128:384], qx[i, pl.ds(al(a * 256, 256), 256), :], (((1,), (1,)), ((), ())),
            preferred_element_type=F32,
        )

    def gather(i, slot, buf):
        scores = buf[...]
        before = m_s[i, 0:1, :]
        peak = jnp.maximum(before, jnp.max(scores, axis=0, keepdims=True))
        m_s[i, 0:1, :] = peak
        weights = jnp.exp2(scores - peak).astype(BF16)
        acc[i] = acc[i] * jnp.exp2(before - peak) + jnp.dot(vt[slot], weights, preferred_element_type=F32)

    def back(i, a):
        rows = pl.ds(a * 256, 256)
        return remote(
            o_stage.at[i, rows, :], mx.at[z, p, rows, :], o_send.at[i, a], o_recv.at[p, a],
            {"seq": me.seq(i, me.gq(i, g))},
        )

    def o_arrive(a):
        rows = pl.ds(a * 256, 256)
        for d in (1, 2, 3):
            h = (p + d) % 4
            arrive(mx.at[z, h, rows, :], o_recv.at[h, a])

        @pl.when(flip == 1)
        def _():
            arrive(mx.at[z, p, rows, :], o_recv.at[p, a])

    def mx_copy(a, direction, k):
        to = zp if direction == 0 else zm
        t, half = ((z, 0), (z, 1), (zm, 0))[k] if direction == 0 else ((z, 1), (z, 0), (zp, 1))[k]
        ref = mx.at[t, :, pl.ds(a * 256 + half * ROWS, ROWS), :]
        return remote(ref, ref, m_send.at[a, direction, k], m_recv.at[a, direction, k], {"tensor": to})

    def mx_arrive(a, direction, k):
        arrive(mx.at[z, :, pl.ds(0, ROWS), :], m_recv.at[a, direction, k])

    def mx_own(a):
        start([mx_copy(a, 0, 0), mx_copy(a, 1, 0), mx_copy(a, 0, 1), mx_copy(a, 1, 1)])

    def mx_relay(a):
        for direction in (0, 1):
            mx_arrive(a, direction, 0)
            mx_copy(a, direction, 2).start()

    def w2_onward():
        for direction in (0, 1):
            arrive(wo.at[pl.ds(0, 192), :], w2_recv.at[direction])
        start(w2_relay())
        start(d2d(1))
        start(d2d(2))

    score(0, 0, 0, s0)
    for a in (0, 1):
        base = 0
        for i in range(4):
            m_s[i] = jnp.full((8, 256), -1e38, F32)
            acc[i] = jnp.zeros((DEPTH, 256), F32)
            count = me.seq(i, me.gq(i, g)) + 1
            steps = (count + 1) // 2

            def two(n, carry):
                if a == 1:
                    pl.when(base + n == HOOKS[0])(lambda: (o_arrive(0), mx_own(0))[0])
                    pl.when(base + n == HOOKS[1])(w2_onward)
                score(i, a, slot_of(2 * n + 1, count), s1)
                gather(i, slot_of(2 * n, count), s0)
                over = (n + 1) // steps
                last = i == 3
                score(
                    ((i + 1) % 4) * over + i * (1 - over), min(a + 1, 1) * over + a * (1 - over) if last else a,
                    (1 - over) * slot_of(2 * n + 2, count), s0,
                )
                gather(i, slot_of(2 * n + 1, count), s1)
                return carry

            lax.fori_loop(0, steps, two, 0)
            base = base + steps
            out = acc[i, 0:128, :] / acc[i, 128:129, :]
            o_stage[i, a * 256 : a * 256 + 256, :] = out.T.astype(BF16)
            stays = (1 - flip) * (p == i).astype(jnp.int32)

            @pl.when(stays == 0)
            def _():
                back(i, a).start()

            @pl.when(stays == 1)
            def _():
                mx[z, p, a * 256 : a * 256 + 256, :] = o_stage[i, a * 256 : a * 256 + 256, :]

    mx_relay(0)
    o_arrive(1)
    mx_own(1)
    for direction in (0, 1):
        arrive(wo.at[pl.ds(0, 96), :], w2r_recv.at[direction])
    start(d2d(3))
    for copy in small_in[1:]:
        copy.wait()
    for direction in (0, 1):
        for k in range(3):
            ref = tok.at[0, halves[0], :]
            remote(ref, ref, ts_sem.at[direction, k], ts_sem.at[direction, k], {"tensor": zp}).wait_send()

    def frame_rows(a):
        for direction in (0, 1):
            for k in (1, 2):
                mx_arrive(a, direction, k)

    def out_project(a):
        rows = pl.ds(a * 256, 256)

        def step(n, carry):
            cols = pl.ds(al(n * 512, 512), 512)
            lhs = jnp.concatenate([mx[t, h, rows, :] for t in range(4) for h in range(4)], axis=1)
            x = jnp.dot(lhs, wo[:, cols], preferred_element_type=F32)
            for k in (0, 1):
                t = 2 * a + k
                tok[t, :, cols] = (tok[t, :, cols].astype(F32) + x[k * ROWS : (k + 1) * ROWS]).astype(BF16)
            return carry

        lax.fori_loop(0, 4, step, 0)
        for k in (0, 1):
            norm_rows(tok.at[2 * a + k], gain2_ref, nrm.at[pl.ds(k * ROWS, ROWS), :], ROWS)

    def up_down(a):
        def up_step(n, carry):
            cols = pl.ds(al(n * 512, 512), 512)
            x = jnp.dot(nrm[...], wu[:, cols], preferred_element_type=F32)
            up[:, cols] = gelu(x).astype(BF16)
            return carry

        lax.fori_loop(0, 4, up_step, 0)

        def down_step(n, carry):
            cols = pl.ds(al(n * 512, 512), 512)
            x = jnp.dot(up[...], wd[:, cols], preferred_element_type=F32)
            fs[a, :, cols] = jnp.sum(x.reshape(32, 8, 512), axis=0)
            for k in (0, 1):
                part[2 * a + k, :, cols] = x[k * ROWS : (k + 1) * ROWS].astype(BF16)
            return carry

        lax.fori_loop(0, 4, down_step, 0)

    lo, hi = halves

    def rs_copy(k):
        src, dst, sem, to = (
            (part.at[z2, lo, :], mid.at[0], mid_recv.at[0], zp),
            (part.at[z2, hi, :], mid.at[1], mid_recv.at[1], zm),
            (part.at[zp, hi, :], fin.at[0, hi, :], fin_recv.at[0, 1], zp),
            (part.at[zm, lo, :], fin.at[1, lo, :], fin_recv.at[1, 0], zm),
            (part.at[zp, lo, :], fin.at[0, lo, :], fin_recv.at[0, 0], zp),
            (part.at[zm, hi, :], fin.at[1, hi, :], fin_recv.at[1, 1], zm),
        )[k]
        return remote(src, dst, rs_send.at[k], sem, {"tensor": to})

    def rs_first(a):
        for t, ks in ((z2, (0, 1)), (zp, (2,)), (zm, (3,))):

            @pl.when(t // 2 == a)
            def _():
                for k in ks:
                    rs_copy(k).start()

    frame_rows(0)
    arrive(wo.at[pl.ds(0, 768), :], d_recv)
    out_project(0)
    mx_relay(1)
    late_in[1].wait()
    late_in[2].wait()
    up_down(0)
    rs_first(0)
    frame_rows(1)
    out_project(1)
    up_down(1)

    def residual(i, total):
        at = pl.ds(al(i * 16, 16), 16)
        return total + jnp.sum(tok[z, at, :].astype(F32).reshape(2, 8, D), axis=0)

    own_rows = lax.fori_loop(0, 8, residual, jnp.zeros((8, D), F32))
    for k in (0, 1):
        mine = (z // 2 == k).astype(F32)
        zs[z, k : k + 1, :] = jnp.sum(fs[k] + own_rows * mine, axis=0, keepdims=True)
    for d in (1, 2, 3):
        send(zs.at[z], zs.at[z], z_send.at[d - 1], z_recv.at[z], {"tensor": (z + d) % 4})
    rs_first(1)
    for d in (1, 2, 3):
        t = (z + d) % 4
        arrive(zs.at[t], z_recv.at[t])
    means[s] = (zs[0] + zs[1] + zs[2] + zs[3]) * (1.0 / TOK_FRAME)
    for d in range(1, 16):
        send(means.at[s], means.at[s], s_send.at[d - 1], s_recv.at[s], {"seq": (s + d) % 16})
    for direction, (t, half) in enumerate(((zp, 0), (zm, 64))):
        arrive(mid.at[direction], mid_recv.at[direction])

        def add(i, carry):
            at = pl.ds(al(i * 16, 16), 16)
            to = pl.ds(al(half + i * 16, 16), 16)
            part[t, to, :] = (part[t, to, :].astype(F32) + mid[direction, at, :].astype(F32)).astype(BF16)
            return carry

        lax.fori_loop(0, 4, add, 0)
        rs_copy(4 + direction).start()

    for d in range(1, 16):
        t = (s + d) % 16
        arrive(means.at[t], s_recv.at[t])
    frame = 2 * lax.broadcasted_iota(jnp.int32, (16, 2, 128), 0) + lax.broadcasted_iota(jnp.int32, (16, 2, 128), 1)
    pg, pb, vw = small[2:3, :], small[3:4, :], small[4:5, :]

    def scan(i, state):
        m = means[i]
        gate = jax.nn.sigmoid(m * pg + pb)
        source = (1.0 - gate) * m
        for k in (0, 1):
            new = gate[k : k + 1] * state + source[k : k + 1]
            state = jnp.where(2 * i + k < length, new, state)
            states[i, k : k + 1, :] = state
        return state

    lax.fori_loop(0, 16, scan, jnp.zeros((1, D), F32))
    total = jnp.sum(states[...] * vw.reshape(1, 1, D), axis=-1, keepdims=True)
    values = jnp.where(frame < length, jnp.broadcast_to(total, (16, 2, 128)), 0.0)
    vals[0] = values
    send(vals.at[0], vals.at[1], v_sem.at[0], v_sem.at[1], {"dp": 1 - c})

    for direction in (0, 1):
        for half, rows in enumerate((lo, hi)):
            arrive(fin.at[direction, rows, :], fin_recv.at[direction, half])

    def output(i, carry):
        at = pl.ds(al(i * 16, 16), 16)
        total = part[z, at, :].astype(F32) + fin[0, at, :].astype(F32) + fin[1, at, :].astype(F32)
        hid_ref[at, :] = (tok[z, at, :].astype(F32) + total).astype(BF16)
        return carry

    lax.fori_loop(0, 8, output, 0)

    arrive(vals.at[1], v_sem.at[1])

    def gaps(v, n):
        valid = frame < n
        reward = jnp.sum(jnp.where(frame == n - 1, v, 0.0), axis=(0, 1), keepdims=True)
        return valid, jnp.where(valid, reward - v, 0.0)

    other = vf_ref[1 - c]
    count = (length + other).astype(F32)
    valid, gap = gaps(values, length)
    valid_o, gap_o = gaps(vals[1], other)
    add = lambda a: jnp.sum(a, axis=(0, 1), keepdims=True)
    mean = (add(gap) + add(gap_o)) / count
    centered = jnp.where(valid, gap - mean, 0.0)
    centered_o = jnp.where(valid_o, gap_o - mean, 0.0)
    variance = (add(centered * centered) + add(centered_o * centered_o)) / count
    adv = jnp.where(valid, centered * lax.rsqrt(variance + 1e-5), 0.0)
    lane = lax.broadcasted_iota(jnp.int32, (1, 128), 1)

    def own_pair(a):
        first = jnp.sum(jnp.where(frame == 2 * s, a, 0.0), axis=(0, 1))
        second = jnp.sum(jnp.where(frame == 2 * s + 1, a, 0.0), axis=(0, 1))
        return jnp.where(lane == 0, first.reshape(1, 128), second.reshape(1, 128))[:, 0:2]

    fv_ref[...] = own_pair(values)
    adv_ref[...] = own_pair(adv)
    @pl.when(flip == 1)
    def _():
        for n in range(4):
            for half, (src, dst) in enumerate(pieces(n)):
                remote(
                    stage.at[n, p, src, third], qx.at[p, dst, lanes],
                    a_send.at[n, 3, 0, half], qs_recv.at[n], {"seq": me.seq(p, 3 - g)},
                ).wait_send()

    for i in range(4):
        stays = (1 - flip) * (p == i).astype(jnp.int32)

        @pl.when(stays == 0)
        def _():
            for a in (0, 1):
                back(i, a).wait_send()

    rest = [w1_copy(d, k) for d in (0, 1) for k in range(3)]
    rest += w2_own() + w2_relay() + [copy for n in range(4) for copy in d2d(n)]
    rest += [mx_copy(a, d, k) for a in (0, 1) for d in (0, 1) for k in range(3)]
    rest += [rs_copy(k) for k in range(6)]
    for copy in rest + sends:
        copy.wait_send()


def local(
    tokens, attn_gain, w_qkv, w_out, mlp_gain, w_up, w_down, pool_gain, pool_bias, value_weight, valid_frames
):
    vmem = pltpu.VMEM
    dma = pltpu.SemaphoreType.DMA
    inside = pl.BlockSpec(memory_space=pltpu.VMEM)
    outside = pl.BlockSpec(memory_space=pl.ANY)
    hidden, values, advantages = pl.pallas_call(
        layer_kernel,
        out_shape=(
            jax.ShapeDtypeStruct((ROWS, D), BF16),
            jax.ShapeDtypeStruct((1, 2), F32),
            jax.ShapeDtypeStruct((1, 2), F32),
        ),
        in_specs=[pl.BlockSpec(memory_space=pltpu.SMEM)] + [outside] * 10,
        out_specs=(inside,) * 3,
        scratch_shapes=[
            vmem((4, ROWS, D), BF16),
            vmem((3, D, BLOCK), BF16),
            vmem((8, D), F32),
            vmem((ROWS, D), BF16),
            vmem((4, 4, ROWS, 384), BF16),
            vmem((4, BLOCK, 256), BF16),
            vmem((17, BLOCK, 384), BF16),
            vmem((17, DEPTH, BLOCK), BF16),
            vmem((4, 8, 256), F32),
            vmem((4, DEPTH, 256), F32),
            vmem((BLOCK, 256), F32),
            vmem((BLOCK, 256), F32),
            vmem((4, BLOCK, HEAD_DIM), BF16),
            vmem((4, 4, BLOCK, HEAD_DIM), BF16),
            vmem((D, D), BF16),
            vmem((D, D), BF16),
            vmem((D, D), BF16),
            vmem((4, ROWS, D), BF16),
            vmem((2, 64, D), BF16),
            vmem((2, ROWS, D), BF16),
            vmem((2 * ROWS, D), BF16),
            vmem((2 * ROWS, D), BF16),
            vmem((2, 8, D), F32),
            vmem((4, 2, D), F32),
            vmem((16, 2, D), F32),
            vmem((16, 2, D), F32),
            vmem((2, 16, 2, 128), F32),
            dma((6,)),
            dma((6,)),
            dma((2, 3)),
            dma((2, 3)),
            dma((4, 4, 2, 2)),
            dma((4,)),
            dma((4,)),
            dma((4,)),
            dma((2, 4, 4)),
            dma((2, 4)),
            dma((4,)),
            dma((4, 2)),
            dma((4, 2)),
            dma((2, 2, 3)),
            dma((2, 2, 3)),
            dma((2, 3)),
            dma((2, 3)),
            dma((2, 5)),
            dma((2,)),
            dma((2,)),
            dma((4, 3)),
            dma,
            dma((6,)),
            dma((2,)),
            dma((2, 2)),
            dma((3,)),
            dma((4,)),
            dma((15,)),
            dma((16,)),
            dma((2,)),
        ],
        compiler_params=pltpu.CompilerParams(
            collective_id=0, has_side_effects=True, vmem_limit_bytes=63 * 2**20
        ),
        cost_estimate=pl.CostEstimate(flops=4 * 10**10, bytes_accessed=4 * 10**7, transcendentals=10**7),
    )(
        valid_frames, tokens[0], w_qkv, w_out, w_up, w_down,
        *(v.reshape(1, D) for v in (attn_gain, mlp_gain, pool_gain, pool_bias, value_weight)),
    )
    return hidden[None], values, advantages


def solution(mesh):
    in_specs = (
        P("dp", ("seq", "tensor"), None),
        P(),
        P(None, None, "tensor"),
        P("tensor", None),
        P(),
        P(None, "tensor"),
        P("tensor", None),
        P(),
        P(),
        P(),
        P(),
    )
    out_specs = (P("dp", ("seq", "tensor"), None), P("dp", "seq"), P("dp", "seq"))
    return jax.shard_map(local, mesh=mesh, in_specs=in_specs, out_specs=out_specs, check_vma=False)
```

time: 145 us -> 122 us (0.84)
  Pallas kernels: 135 us -> 117 us
  local copies, waits for them, and re-layouts: 7.4 us -> 4.17 us
    pallas_call x2 -> x1, Pallas kernels: 135 us -> 117 us  [local(): pl.pallas_call(layer_kernel, out_shape=(jax.ShapeDtypeStruct((ROWS, D), B...]
    unnamed x11 -> x3, local copies, waits for them, and re-layouts: 7.4 us -> 4.17 us
where the time goes in v4:
time: 122 us
  Pallas kernels  117 us (96%)
  local copies, waits for them, and re-layouts  4.17 us (3%)
    pallas_call x1, Pallas kernels, local(): pl.pallas_call(layer_kernel, out_shape=(jax.ShapeDtypeStruct((ROWS, D), B...  117 us
    unnamed x3, local copies, waits for them, and re-layouts  4.17 us

profile of v4, /device:TPU:1, one launch (start us, length us, event | category | flops | bytes accessed | tf_op | source)
XLA Modules:
  0.0 121.6 jit_solution(14120270295077318634)
XLA Ops:
  0.6 116.7 %shard_map.130 = (bf16[128,2048]{1,0:T(8,128)(2,1)}, f32[1,2]{1,0:T(1,128)}, f32[1,2]{1,0:T(1,128)}) custom-call(s32[2]{0:T(128)} %vf_ref.1, bf16[128,2048]{1,0:T(8,128)(2,1)} %bitcast.8, bf16[3,2048,512]{2,1,0:T(8,128)(2,1)} %w_hbm.1, bf16[512,2048]{1,0:T(8,128)(2,1)} %wo_hbm.1, bf16[2048,2048]{1,0:T(8,128)(2,1)} %wu_hbm.1, bf16[2048,2048]{1,0:T(8,128)(2,1)} %wd_hbm.1, ...), custom_call_target="tpu_custom_call" | custom-call | flops 40000000000 | bytes 40000000 | tf_op jit(solution)/shard_map/pallas_call | solution.py:661
  117.4 1.9 %copy.17 = bf16[1,128,2048]{2,1,0:T(8,128)(2,1)} copy(bf16[1,128,2048]{2,1,0:T(8,128)(2,1)} %bitcast.7) | data formatting | bytes 1048576
  119.3 1.1 copy.18
  120.4 1.2 copy.19

commit v5 on v4

--- a/solution.py
+++ b/solution.py
@@ -21,7 +21,8 @@
 QSCALE = math.log2(math.e) / math.sqrt(HEAD_DIM)
 NEG = -1e30
 ONWARD = (0, 1)
-HOOKS = (9, 11)
+HOOKS = (8, 12, 28)
+UNROLL = 4
 
 
 def remote(src, dst, send_sem, recv_sem, where):
@@ -158,14 +159,19 @@
                 stage[n, 2 * pair, :, at] = out[:, :128]
                 stage[n, 2 * pair + 1, :, at] = out[:, 128:]
 
+    def query_rows(piece, count):
+        t, half = piece
+        return pl.ds(al((t % 2) * 256 + (t // 2) * ROWS + half * HALF, HALF), count)
+
     both = pl.ds(0, 256)
     third = pl.ds(256, 128)
     lanes = pl.ds(0, HEAD_DIM)
 
     def pieces(n):
         if n in (0, 3):
-            return ((pl.ds(0, ROWS), pl.ds(al(stages[n][0][0] * ROWS, ROWS), ROWS)),)
-        return tuple((halves[k], rows_of(piece)) for k, piece in enumerate(stages[n]))
+            piece = stages[n][0]
+            return ((pl.ds(0, ROWS), pl.ds(al(piece[0] * ROWS, ROWS), ROWS), query_rows(piece, ROWS)),)
+        return tuple((halves[k], rows_of(piece), query_rows(piece, HALF)) for k, piece in enumerate(stages[n]))
 
     def hand_out(n):
         for k, (buf, sem, part) in enumerate(((kx, k_recv, both), (qx, q_recv, third))):
@@ -173,17 +179,17 @@
                 h = (p + d) % 4
                 to = {"seq": me.seq(h, me.gq(p, g) if k else g)}
                 slot = p if k else g * 4 + p
-                for half, (src, dst) in enumerate(pieces(n)):
+                for half, (src, dst, dst_q) in enumerate(pieces(n)):
                     send(
-                        stage.at[n, h, src, part], buf.at[slot, dst, lanes if k else both],
+                        stage.at[n, h, src, part], buf.at[slot, dst_q if k else dst, lanes if k else both],
                         a_send.at[n, d - 1, k, half], sem.at[n], to,
                     )
-        for src, dst in pieces(n):
+        for src, dst, _ in pieces(n):
             kx[g * 4 + p, dst, 0:256] = stage[n, p, src, 0:256]
 
         @pl.when(flip == 1)
         def _():
-            for half, (src, dst) in enumerate(pieces(n)):
+            for half, (src, _, dst) in enumerate(pieces(n)):
                 remote(
                     stage.at[n, p, src, third], qx.at[p, dst, lanes],
                     a_send.at[n, 3, 0, half], qs_recv.at[n], {"seq": me.seq(p, 3 - g)},
@@ -191,7 +197,7 @@
 
         @pl.when(flip == 0)
         def _():
-            for src, dst in pieces(n):
+            for src, _, dst in pieces(n):
                 qx[p, dst, 0:128] = stage[n, p, src, 256:384]
 
     def stage_in(count, buf, sem):
@@ -201,7 +207,7 @@
         stage_in(3, kx, k_recv.at[n])
         for direction in (0, 1):
             to = {"seq": me.seq(p, gp if direction == 0 else gm)}
-            for half, (_, dst) in enumerate(pieces(n)):
+            for half, (_, dst, _) in enumerate(pieces(n)):
                 ref = kx.at[pl.ds(g * 4, 4), dst, both]
                 send(ref, ref, g_send.at[direction, n, half], gk_recv.at[direction, n], to)
 
@@ -212,8 +218,8 @@
             if ONWARD[0] == ONWARD[1]:
                 runs = pieces(n)
             else:
-                runs = ((0, rows_of(stages[n][direction])),)
-            for half, (_, dst) in enumerate(runs):
+                runs = ((0, rows_of(stages[n][direction]), 0),)
+            for half, (_, dst, _) in enumerate(runs):
                 ref = kx.at[pl.ds(source * 4, 4), dst, both]
                 send(ref, ref, g_send.at[direction, n, 2 + half], r_recv.at[n], {"seq": me.seq(p, to)})
 
@@ -292,7 +298,7 @@
     kx[16, :, 256:384] = jnp.where(lane == 0, NEG, 0.0).astype(BF16)
     vt[16] = jnp.zeros((DEPTH, BLOCK), BF16)
     for i in range(4):
-        on = (lane == 0) | ((lane == 1 + i) & (row < TOK_FRAME))
+        on = (lane == 0) | ((lane == 1 + i) & (row % 256 < ROWS))
         qx[i, :, 128:256] = jnp.where(on, 1.0, 0.0).astype(BF16)
 
     tok_wait(0, 0, zm, 0)
@@ -339,6 +345,11 @@
     turn(g)
     relay(3)
     for direction in (0, 1):
+        for k in (1, 2):
+            w1_arrive(direction, k)
+    start(w2_own())
+    start(d2d(0))
+    for direction in (0, 1):
         if direction not in ONWARD:
             for n in range(4):
                 stage_in(4, kx, gk_recv.at[direction, n])
@@ -347,30 +358,58 @@
     for n in range(4):
         stage_in(4, kx, r_recv.at[n])
     turn(g2)
-    for direction in (0, 1):
-        for k in (1, 2):
-            w1_arrive(direction, k)
-    start(w2_own())
-    start(d2d(0))
 
     def slot_of(b, count):
         pad = b // count
         slot = (1 - c) * ((b % 4) * 4 + b // 4) + c * b
         return (1 - pad) * slot + pad * 16
 
-    def score(i, a, slot, buf):
-        buf[...] = lax.dot_general(
-            kx[slot, :, 128:384], qx[i, pl.ds(al(a * 256, 256), 256), :], (((1,), (1,)), ((), ())),
-            preferred_element_type=F32,
-        )
-
-    def gather(i, slot, buf):
-        scores = buf[...]
-        before = m_s[i, 0:1, :]
-        peak = jnp.maximum(before, jnp.max(scores, axis=0, keepdims=True))
-        m_s[i, 0:1, :] = peak
-        weights = jnp.exp2(scores - peak).astype(BF16)
-        acc[i] = acc[i] * jnp.exp2(before - peak) + jnp.dot(vt[slot], weights, preferred_element_type=F32)
+    counts = [me.seq(i, me.gq(i, g)) + 1 for i in range(4)]
+    first = [0]
+    for count in counts:
+        first.append(first[-1] + (count + 1) // 2)
+    turns = first[4]
+
+    def pick(at_i, choices):
+        return sum(((at_i == k).astype(jnp.int32) * value for k, value in enumerate(choices)), 0)
+
+    def unit(u):
+        past = u // (2 * turns)
+        u = u - past * (u - 2 * turns + 1)
+        a, v = u // turns, u % turns
+        i = sum(((v >= first[k]).astype(jnp.int32) for k in (1, 2, 3)), 0)
+        j = v - pick(i, first[:4])
+        count = pick(i, counts)
+        return a, i, [
+            (1 - past) * slot_of(2 * j + k, count) + past * 16 for k in (0, 1)
+        ]
+
+    def score(u):
+        a, i, slots = unit(u)
+        for k, slot in enumerate(slots):
+            s0[k * BLOCK : (k + 1) * BLOCK, :] = lax.dot_general(
+                kx[slot, :, 128:384], qx[i, pl.ds(al(a * 256, 256), 256), :], (((1,), (1,)), ((), ())),
+                preferred_element_type=F32,
+            )
+
+    def soften(u):
+        a, i, _ = unit(u)
+        before = m_s[a * 4 + i, 0:1, :]
+        peak = jnp.full((8, 256), -1e38, F32)
+        for r in range(0, 2 * BLOCK, 128):
+            peak = jnp.maximum(peak, jnp.max(s0[r : r + 128, :].reshape(16, 8, 256), axis=0))
+        peak = jnp.maximum(before, jnp.max(peak, axis=0, keepdims=True))
+        m_s[a * 4 + i, 0:1, :] = peak
+        m_s[8, 0:1, :] = jnp.exp2(before - peak)
+        for r in range(0, 2 * BLOCK, 128):
+            s1[r : r + 128, :] = jnp.exp2(s0[r : r + 128, :] - peak).astype(BF16)
+
+    def gather(u):
+        a, i, slots = unit(u)
+        out = acc[a * 4 + i] * m_s[8, 0:1, :]
+        for k, slot in enumerate(slots):
+            out = out + jnp.dot(vt[slot], s1[k * BLOCK : (k + 1) * BLOCK, :], preferred_element_type=F32)
+        acc[a * 4 + i] = out
 
     def back(i, a):
         rows = pl.ds(a * 256, 256)
@@ -413,34 +452,11 @@
         start(d2d(1))
         start(d2d(2))
 
-    score(0, 0, 0, s0)
-    for a in (0, 1):
-        base = 0
+    def give_back(a):
         for i in range(4):
-            m_s[i] = jnp.full((8, 256), -1e38, F32)
-            acc[i] = jnp.zeros((DEPTH, 256), F32)
-            count = me.seq(i, me.gq(i, g)) + 1
-            steps = (count + 1) // 2
-
-            def two(n, carry):
-                if a == 1:
-                    pl.when(base + n == HOOKS[0])(lambda: (o_arrive(0), mx_own(0))[0])
-                    pl.when(base + n == HOOKS[1])(w2_onward)
-                score(i, a, slot_of(2 * n + 1, count), s1)
-                gather(i, slot_of(2 * n, count), s0)
-                over = (n + 1) // steps
-                last = i == 3
-                score(
-                    ((i + 1) % 4) * over + i * (1 - over), min(a + 1, 1) * over + a * (1 - over) if last else a,
-                    (1 - over) * slot_of(2 * n + 2, count), s0,
-                )
-                gather(i, slot_of(2 * n + 1, count), s1)
-                return carry
-
-            lax.fori_loop(0, steps, two, 0)
-            base = base + steps
-            out = acc[i, 0:128, :] / acc[i, 128:129, :]
-            o_stage[i, a * 256 : a * 256 + 256, :] = out.T.astype(BF16)
+            rows = pl.ds(a * 256, 256)
+            out = acc[a * 4 + i, 0:128, :] / acc[a * 4 + i, 128:129, :]
+            o_stage[i, rows, :] = out.T.astype(BF16)
             stays = (1 - flip) * (p == i).astype(jnp.int32)
 
             @pl.when(stays == 0)
@@ -449,14 +465,47 @@
 
             @pl.when(stays == 1)
             def _():
-                mx[z, p, a * 256 : a * 256 + 256, :] = o_stage[i, a * 256 : a * 256 + 256, :]
+                mx[z, p, rows, :] = o_stage[i, rows, :]
+
+    for k in range(8):
+        m_s[k] = jnp.full((8, 256), -1e38, F32)
+        acc[k] = jnp.zeros((DEPTH, 256), F32)
+    def w2_last():
+        for direction in (0, 1):
+            arrive(wo.at[pl.ds(0, 96), :], w2r_recv.at[direction])
+        start(d2d(3))
+
+    score(0)
+    soften(0)
+    score(1)
+
+    per = UNROLL
+    half_way = (turns + per - 1) // per
+
+    def turn_step(n, carry):
+        @pl.when(n == half_way)
+        def _():
+            give_back(0)
+
+        @pl.when(n == half_way + HOOKS[0] // per)
+        def _():
+            o_arrive(0)
+            mx_own(0)
+
+        pl.when(n == HOOKS[1] // per)(w2_onward)
+        pl.when(n == HOOKS[2] // per)(w2_last)
+        for k in range(per):
+            gather(n * per + k)
+            soften(n * per + k + 1)
+            score(n * per + k + 2)
+        return carry
+
+    lax.fori_loop(0, (2 * turns + per - 1) // per, turn_step, 0)
+    give_back(1)
 
     mx_relay(0)
     o_arrive(1)
     mx_own(1)
-    for direction in (0, 1):
-        arrive(wo.at[pl.ds(0, 96), :], w2r_recv.at[direction])
-    start(d2d(3))
     for copy in small_in[1:]:
         copy.wait()
     for direction in (0, 1):
@@ -477,15 +526,41 @@
             lhs = jnp.concatenate([mx[t, h, rows, :] for t in range(4) for h in range(4)], axis=1)
             x = jnp.dot(lhs, wo[:, cols], preferred_element_type=F32)
             for k in (0, 1):
-                t = 2 * a + k
+                t = a + 2 * k
                 tok[t, :, cols] = (tok[t, :, cols].astype(F32) + x[k * ROWS : (k + 1) * ROWS]).astype(BF16)
             return carry
 
         lax.fori_loop(0, 4, step, 0)
         for k in (0, 1):
-            norm_rows(tok.at[2 * a + k], gain2_ref, nrm.at[pl.ds(k * ROWS, ROWS), :], ROWS)
-
-    def up_down(a):
+            norm_rows(tok.at[a + 2 * k], gain2_ref, nrm.at[pl.ds(k * ROWS, ROWS), :], ROWS)
+
+    lo, hi = halves
+    ways = ((zp, lo, hi), (zm, hi, lo))
+
+    def mid_copy(direction, n):
+        to, rows, _ = ways[direction]
+        cols = pl.ds(n * 512, 512)
+        return remote(
+            part.at[z2, rows, cols], mid.at[direction, :, cols], rs_send.at[direction, n],
+            mid_recv.at[direction, n], {"tensor": to},
+        )
+
+    def direct_copy(direction):
+        to, _, rows = ways[direction]
+        return remote(
+            part.at[to, rows, :], fin.at[direction, rows, :], rs_send.at[direction, 4],
+            fin_recv.at[direction, 0], {"tensor": to},
+        )
+
+    def sum_copy(direction, n):
+        to, rows, _ = ways[direction]
+        cols = pl.ds(n * 512, 512)
+        return remote(
+            part.at[to, rows, cols], fin.at[direction, rows, cols], rs_send.at[direction, 5 + n],
+            fin_recv.at[direction, 1], {"tensor": to},
+        )
+
+    def up_down(a, between=lambda: None):
         def up_step(n, carry):
             cols = pl.ds(al(n * 512, 512), 512)
             x = jnp.dot(nrm[...], wu[:, cols], preferred_element_type=F32)
@@ -494,36 +569,41 @@
 
         lax.fori_loop(0, 4, up_step, 0)
 
-        def down_step(n, carry):
-            cols = pl.ds(al(n * 512, 512), 512)
+        for n in range(4):
+            cols = slice(n * 512, n * 512 + 512)
             x = jnp.dot(up[...], wd[:, cols], preferred_element_type=F32)
-            fs[a, :, cols] = jnp.sum(x.reshape(32, 8, 512), axis=0)
             for k in (0, 1):
-                part[2 * a + k, :, cols] = x[k * ROWS : (k + 1) * ROWS].astype(BF16)
-            return carry
-
-        lax.fori_loop(0, 4, down_step, 0)
-
-    lo, hi = halves
-
-    def rs_copy(k):
-        src, dst, sem, to = (
-            (part.at[z2, lo, :], mid.at[0], mid_recv.at[0], zp),
-            (part.at[z2, hi, :], mid.at[1], mid_recv.at[1], zm),
-            (part.at[zp, hi, :], fin.at[0, hi, :], fin_recv.at[0, 1], zp),
-            (part.at[zm, lo, :], fin.at[1, lo, :], fin_recv.at[1, 0], zm),
-            (part.at[zp, lo, :], fin.at[0, lo, :], fin_recv.at[0, 0], zp),
-            (part.at[zm, hi, :], fin.at[1, hi, :], fin_recv.at[1, 1], zm),
-        )[k]
-        return remote(src, dst, rs_send.at[k], sem, {"tensor": to})
+                rows = x[k * ROWS : (k + 1) * ROWS]
+                part[a + 2 * k, :, cols] = rows.astype(BF16)
+                rows = jnp.sum(rows.reshape(16, 8, 512), axis=0)
+                fs[k, :, cols] = fs[k, :, cols] + rows if a else rows
+            if n == 3:
+                between()
+
+            @pl.when(z2 % 2 == a)
+            def _():
+                for direction in (0, 1):
+                    mid_copy(direction, n).start()
 
     def rs_first(a):
-        for t, ks in ((z2, (0, 1)), (zp, (2,)), (zm, (3,))):
-
-            @pl.when(t // 2 == a)
+        for t, direction in ((zp, 0), (zm, 1)):
+
+            @pl.when(t % 2 == a)
             def _():
-                for k in ks:
-                    rs_copy(k).start()
+                direct_copy(direction).start()
+
+    def rs_sums(a):
+        @pl.when(zp % 2 == a)
+        def _():
+            for n in range(4):
+                cols = slice(n * 512, n * 512 + 512)
+                for direction, (t, half) in enumerate(((zp, 0), (zm, 64))):
+                    arrive(mid.at[direction, :, pl.ds(n * 512, 512)], mid_recv.at[direction, n])
+                    rows = slice(half, half + 64)
+                    part[t, rows, cols] = (
+                        part[t, rows, cols].astype(F32) + mid[direction, :, cols].astype(F32)
+                    ).astype(BF16)
+                    sum_copy(direction, n).start()
 
     frame_rows(0)
     arrive(wo.at[pl.ds(0, 768), :], d_recv)
@@ -535,18 +615,21 @@
     rs_first(0)
     frame_rows(1)
     out_project(1)
-    up_down(1)
-
     def residual(i, total):
         at = pl.ds(al(i * 16, 16), 16)
         return total + jnp.sum(tok[z, at, :].astype(F32).reshape(2, 8, D), axis=0)
 
-    own_rows = lax.fori_loop(0, 8, residual, jnp.zeros((8, D), F32))
-    for k in (0, 1):
-        mine = (z // 2 == k).astype(F32)
-        zs[z, k : k + 1, :] = jnp.sum(fs[k] + own_rows * mine, axis=0, keepdims=True)
-    for d in (1, 2, 3):
-        send(zs.at[z], zs.at[z], z_send.at[d - 1], z_recv.at[z], {"tensor": (z + d) % 4})
+    fs[2] = lax.fori_loop(0, 8, residual, jnp.zeros((8, D), F32))
+
+    def sums_out():
+        for k in (0, 1):
+            mine = (z // 2 == k).astype(F32)
+            zs[z, k : k + 1, :] = jnp.sum(fs[k] + fs[2] * mine, axis=0, keepdims=True)
+        for d in (1, 2, 3):
+            send(zs.at[z], zs.at[z], z_send.at[d - 1], z_recv.at[z], {"tensor": (z + d) % 4})
+
+    rs_sums(0)
+    up_down(1, sums_out)
     rs_first(1)
     for d in (1, 2, 3):
         t = (z + d) % 4
@@ -554,18 +637,7 @@
     means[s] = (zs[0] + zs[1] + zs[2] + zs[3]) * (1.0 / TOK_FRAME)
     for d in range(1, 16):
         send(means.at[s], means.at[s], s_send.at[d - 1], s_recv.at[s], {"seq": (s + d) % 16})
-    for direction, (t, half) in enumerate(((zp, 0), (zm, 64))):
-        arrive(mid.at[direction], mid_recv.at[direction])
-
-        def add(i, carry):
-            at = pl.ds(al(i * 16, 16), 16)
-            to = pl.ds(al(half + i * 16, 16), 16)
-            part[t, to, :] = (part[t, to, :].astype(F32) + mid[direction, at, :].astype(F32)).astype(BF16)
-            return carry
-
-        lax.fori_loop(0, 4, add, 0)
-        rs_copy(4 + direction).start()
-
+    rs_sums(1)
     for d in range(1, 16):
         t = (s + d) % 16
         arrive(means.at[t], s_recv.at[t])
@@ -589,8 +661,8 @@
     send(vals.at[0], vals.at[1], v_sem.at[0], v_sem.at[1], {"dp": 1 - c})
 
     for direction in (0, 1):
-        for half, rows in enumerate((lo, hi)):
-            arrive(fin.at[direction, rows, :], fin_recv.at[direction, half])
+        for k in (0, 1):
+            arrive(fin.at[direction, lo, :], fin_recv.at[direction, k])
 
     def output(i, carry):
         at = pl.ds(al(i * 16, 16), 16)
@@ -629,7 +701,7 @@
     @pl.when(flip == 1)
     def _():
         for n in range(4):
-            for half, (src, dst) in enumerate(pieces(n)):
+            for half, (src, _, dst) in enumerate(pieces(n)):
                 remote(
                     stage.at[n, p, src, third], qx.at[p, dst, lanes],
                     a_send.at[n, 3, 0, half], qs_recv.at[n], {"seq": me.seq(p, 3 - g)},
@@ -646,7 +718,8 @@
     rest = [w1_copy(d, k) for d in (0, 1) for k in range(3)]
     rest += w2_own() + w2_relay() + [copy for n in range(4) for copy in d2d(n)]
     rest += [mx_copy(a, d, k) for a in (0, 1) for d in (0, 1) for k in range(3)]
-    rest += [rs_copy(k) for k in range(6)]
+    for d in (0, 1):
+        rest += [direct_copy(d)] + [copy(d, n) for copy in (mid_copy, sum_copy) for n in range(4)]
     for copy in rest + sends:
         copy.wait_send()
 
@@ -676,10 +749,10 @@
             vmem((4, BLOCK, 256), BF16),
             vmem((17, BLOCK, 384), BF16),
             vmem((17, DEPTH, BLOCK), BF16),
-            vmem((4, 8, 256), F32),
-            vmem((4, DEPTH, 256), F32),
-            vmem((BLOCK, 256), F32),
-            vmem((BLOCK, 256), F32),
+            vmem((9, 8, 256), F32),
+            vmem((8, DEPTH, 256), F32),
+            vmem((2 * BLOCK, 256), F32),
+            vmem((2 * BLOCK, 256), BF16),
             vmem((4, BLOCK, HEAD_DIM), BF16),
             vmem((4, 4, BLOCK, HEAD_DIM), BF16),
             vmem((D, D), BF16),
@@ -690,7 +763,7 @@
             vmem((2, ROWS, D), BF16),
             vmem((2 * ROWS, D), BF16),
             vmem((2 * ROWS, D), BF16),
-            vmem((2, 8, D), F32),
+            vmem((3, 8, D), F32),
             vmem((4, 2, D), F32),
             vmem((16, 2, D), F32),
             vmem((16, 2, D), F32),
@@ -717,8 +790,8 @@
             dma((2,)),
             dma((4, 3)),
             dma,
-            dma((6,)),
-            dma((2,)),
+            dma((2, 9)),
+            dma((2, 4)),
             dma((2, 2)),
             dma((3,)),
             dma((4,)),

time: 122 us -> 119 us (0.975)
  Pallas kernels: 117 us -> 114 us
    pallas_call x1, Pallas kernels: 117 us -> 114 us  [local(): pl.pallas_call(layer_kernel, out_shape=(jax.ShapeDtypeStruct((ROWS, D), B...]
where the time goes in v5:
time: 119 us
  Pallas kernels  114 us (96%)
  local copies, waits for them, and re-layouts  4.17 us (4%)
    pallas_call x1, Pallas kernels, local(): pl.pallas_call(layer_kernel, out_shape=(jax.ShapeDtypeStruct((ROWS, D), B...  114 us
    unnamed x3, local copies, waits for them, and re-layouts  4.17 us

profile of v5, /device:TPU:1, one launch (start us, length us, event | category | flops | bytes accessed | tf_op | source)
XLA Modules:
  0.0 119.0 jit_solution(14684574435232223451)
XLA Ops:
  0.6 114.2 %shard_map.130 = (bf16[128,2048]{1,0:T(8,128)(2,1)}, f32[1,2]{1,0:T(1,128)}, f32[1,2]{1,0:T(1,128)}) custom-call(s32[2]{0:T(128)} %vf_ref.1, bf16[128,2048]{1,0:T(8,128)(2,1)} %bitcast.8, bf16[3,2048,512]{2,1,0:T(8,128)(2,1)} %w_hbm.1, bf16[512,2048]{1,0:T(8,128)(2,1)} %wo_hbm.1, bf16[2048,2048]{1,0:T(8,128)(2,1)} %wu_hbm.1, bf16[2048,2048]{1,0:T(8,128)(2,1)} %wd_hbm.1, ...), custom_call_target="tpu_custom_call" | custom-call | flops 40000000000 | bytes 40000000 | tf_op jit(solution)/shard_map/pallas_call | solution.py:734
  114.9 1.9 %copy.17 = bf16[1,128,2048]{2,1,0:T(8,128)(2,1)} copy(bf16[1,128,2048]{2,1,0:T(8,128)(2,1)} %bitcast.7) | data formatting | bytes 1048576
  116.8 1.1 copy.18
  117.9 1.2 copy.19

commit v6 on v5

--- a/solution.py
+++ b/solution.py
@@ -21,7 +21,7 @@
 QSCALE = math.log2(math.e) / math.sqrt(HEAD_DIM)
 NEG = -1e30
 ONWARD = (0, 1)
-HOOKS = (8, 12, 28)
+HOOKS = (12, 20)
 UNROLL = 4
 
 
@@ -360,9 +360,9 @@
     turn(g2)
 
     def slot_of(b, count):
-        pad = b // count
-        slot = (1 - c) * ((b % 4) * 4 + b // 4) + c * b
-        return (1 - pad) * slot + pad * 16
+        pad = (b >= count).astype(jnp.int32)
+        slot = (1 - c) * (lax.rem(b, 4) * 4 + lax.div(b, 4)) + c * b
+        return slot + pad * (16 - slot)
 
     counts = [me.seq(i, me.gq(i, g)) + 1 for i in range(4)]
     first = [0]
@@ -374,26 +374,26 @@
         return sum(((at_i == k).astype(jnp.int32) * value for k, value in enumerate(choices)), 0)
 
     def unit(u):
-        past = u // (2 * turns)
+        past = (u >= 2 * turns).astype(jnp.int32)
         u = u - past * (u - 2 * turns + 1)
-        a, v = u // turns, u % turns
+        a = (u >= turns).astype(jnp.int32)
+        v = u - a * turns
         i = sum(((v >= first[k]).astype(jnp.int32) for k in (1, 2, 3)), 0)
         j = v - pick(i, first[:4])
         count = pick(i, counts)
-        return a, i, [
-            (1 - past) * slot_of(2 * j + k, count) + past * 16 for k in (0, 1)
-        ]
-
-    def score(u):
-        a, i, slots = unit(u)
+        slots = tuple(slot + past * (16 - slot) for slot in (slot_of(2 * j, count), slot_of(2 * j + 1, count)))
+        return a, i, *slots
+
+    def score(now):
+        a, i, *slots = now
         for k, slot in enumerate(slots):
             s0[k * BLOCK : (k + 1) * BLOCK, :] = lax.dot_general(
                 kx[slot, :, 128:384], qx[i, pl.ds(al(a * 256, 256), 256), :], (((1,), (1,)), ((), ())),
                 preferred_element_type=F32,
             )
 
-    def soften(u):
-        a, i, _ = unit(u)
+    def soften(now):
+        a, i, *_ = now
         before = m_s[a * 4 + i, 0:1, :]
         peak = jnp.full((8, 256), -1e38, F32)
         for r in range(0, 2 * BLOCK, 128):
@@ -404,8 +404,8 @@
         for r in range(0, 2 * BLOCK, 128):
             s1[r : r + 128, :] = jnp.exp2(s0[r : r + 128, :] - peak).astype(BF16)
 
-    def gather(u):
-        a, i, slots = unit(u)
+    def gather(now):
+        a, i, *slots = now
         out = acc[a * 4 + i] * m_s[8, 0:1, :]
         for k, slot in enumerate(slots):
             out = out + jnp.dot(vt[slot], s1[k * BLOCK : (k + 1) * BLOCK, :], preferred_element_type=F32)
@@ -475,9 +475,9 @@
             arrive(wo.at[pl.ds(0, 96), :], w2r_recv.at[direction])
         start(d2d(3))
 
-    score(0)
-    soften(0)
-    score(1)
+    score(unit(0))
+    soften(unit(0))
+    score(unit(1))
 
     per = UNROLL
     half_way = (turns + per - 1) // per
@@ -493,17 +493,18 @@
             mx_own(0)
 
         pl.when(n == HOOKS[1] // per)(w2_onward)
-        pl.when(n == HOOKS[2] // per)(w2_last)
+        units = [*carry, *(unit((n + 1) * per + k) for k in (2, *range(3, per + 2)))]
         for k in range(per):
-            gather(n * per + k)
-            soften(n * per + k + 1)
-            score(n * per + k + 2)
-        return carry
-
-    lax.fori_loop(0, (2 * turns + per - 1) // per, turn_step, 0)
+            gather(carry[k])
+            soften(carry[k + 1])
+            score(carry[k + 2])
+        return tuple(units[per:])
+
+    lax.fori_loop(0, (2 * turns + per - 1) // per, turn_step, tuple(unit(k) for k in range(per + 2)))
     give_back(1)
 
     mx_relay(0)
+    w2_last()
     o_arrive(1)
     mx_own(1)
     for copy in small_in[1:]:
@@ -521,16 +522,13 @@
     def out_project(a):
         rows = pl.ds(a * 256, 256)
 
-        def step(n, carry):
-            cols = pl.ds(al(n * 512, 512), 512)
+        for n in range(4):
+            cols = slice(n * 512, n * 512 + 512)
             lhs = jnp.concatenate([mx[t, h, rows, :] for t in range(4) for h in range(4)], axis=1)
             x = jnp.dot(lhs, wo[:, cols], preferred_element_type=F32)
             for k in (0, 1):
                 t = a + 2 * k
                 tok[t, :, cols] = (tok[t, :, cols].astype(F32) + x[k * ROWS : (k + 1) * ROWS]).astype(BF16)
-            return carry
-
-        lax.fori_loop(0, 4, step, 0)
         for k in (0, 1):
             norm_rows(tok.at[a + 2 * k], gain2_ref, nrm.at[pl.ds(k * ROWS, ROWS), :], ROWS)
 
@@ -561,13 +559,10 @@
         )
 
     def up_down(a, between=lambda: None):
-        def up_step(n, carry):
-            cols = pl.ds(al(n * 512, 512), 512)
+        for n in range(4):
+            cols = slice(n * 512, n * 512 + 512)
             x = jnp.dot(nrm[...], wu[:, cols], preferred_element_type=F32)
             up[:, cols] = gelu(x).astype(BF16)
-            return carry
-
-        lax.fori_loop(0, 4, up_step, 0)
 
         for n in range(4):
             cols = slice(n * 512, n * 512 + 512)
@@ -579,11 +574,14 @@
                 fs[k, :, cols] = fs[k, :, cols] + rows if a else rows
             if n == 3:
                 between()
+            if a == 1 and n < 3:
+                continue
 
             @pl.when(z2 % 2 == a)
             def _():
-                for direction in (0, 1):
-                    mid_copy(direction, n).start()
+                for m in range(4) if a else (n,):
+                    for direction in (0, 1):
+                        mid_copy(direction, m).start()
 
     def rs_first(a):
         for t, direction in ((zp, 0), (zm, 1)):
@@ -722,6 +720,18 @@
         rest += [direct_copy(d)] + [copy(d, n) for copy in (mid_copy, sum_copy) for n in range(4)]
     for copy in rest + sends:
         copy.wait_send()
+
+
+def hand_over(hid_ref, fv_ref, adv_ref, hid_out, fv_out, adv_out, sem):
+    copies = [
+        pltpu.make_async_copy(hid_ref, hid_out.at[0], sem.at[0]),
+        pltpu.make_async_copy(fv_ref, fv_out, sem.at[1]),
+        pltpu.make_async_copy(adv_ref, adv_out, sem.at[2]),
+    ]
+    for copy in copies:
+        copy.start()
+    for copy in copies:
+        copy.wait()
 
 
 def local(
@@ -807,7 +817,17 @@
         valid_frames, tokens[0], w_qkv, w_out, w_up, w_down,
         *(v.reshape(1, D) for v in (attn_gain, mlp_gain, pool_gain, pool_bias, value_weight)),
     )
-    return hidden[None], values, advantages
+    return pl.pallas_call(
+        hand_over,
+        out_shape=(
+            jax.ShapeDtypeStruct((1, ROWS, D), BF16),
+            jax.ShapeDtypeStruct((1, 2), F32),
+            jax.ShapeDtypeStruct((1, 2), F32),
+        ),
+        in_specs=[inside] * 3,
+        out_specs=(outside,) * 3,
+        scratch_shapes=[dma((3,))],
+    )(hidden, values, advantages)
 
 
 def solution(mesh):

time: 119 us -> 109 us (0.916)
  Pallas kernels: 114 us -> 108 us
  local copies, waits for them, and re-layouts: 4.17 us -> 0 us
    pallas_call x1, Pallas kernels: 114 us -> 106 us  [local(): pl.pallas_call(layer_kernel, out_shape=(jax.ShapeDtypeStruct((ROWS, D), B...]
    unnamed x3 -> x0, local copies, waits for them, and re-layouts: 4.17 us -> none
    pallas_call x0 -> x1, Pallas kernels: none -> 1.87 us  [local(): pl.pallas_call(hand_over, out_shape=(jax.ShapeDtypeStruct((1, ROWS, D), B...]
where the time goes in v6:
time: 109 us
  Pallas kernels  108 us (99%)
    pallas_call x1, Pallas kernels, local(): pl.pallas_call(layer_kernel, out_shape=(jax.ShapeDtypeStruct((ROWS, D), B...  106 us

profile of v6, /device:TPU:1, one launch (start us, length us, event | category | flops | bytes accessed | tf_op | source)
XLA Modules:
  0.0 108.8 jit_solution(5198594031890599229)
XLA Ops:
  0.6 106.2 %shard_map.130 = (bf16[128,2048]{1,0:T(8,128)(2,1)}, f32[1,2]{1,0:T(1,128)}, f32[1,2]{1,0:T(1,128)}) custom-call(s32[2]{0:T(128)} %vf_ref.1, bf16[128,2048]{1,0:T(8,128)(2,1)} %bitcast.6, bf16[3,2048,512]{2,1,0:T(8,128)(2,1)} %w_hbm.1, bf16[512,2048]{1,0:T(8,128)(2,1)} %wo_hbm.1, bf16[2048,2048]{1,0:T(8,128)(2,1)} %wu_hbm.1, bf16[2048,2048]{1,0:T(8,128)(2,1)} %wd_hbm.1, ...), custom_call_target="tpu_custom_call" | custom-call | flops 40000000000 | bytes 40000000 | tf_op jit(solution)/shard_map/pallas_call | solution.py:744
  106.8 1.9 %shard_map.131 = (bf16[1,128,2048]{2,1,0:T(8,128)(2,1)}, f32[1,2]{1,0:T(1,128)}, f32[1,2]{1,0:T(1,128)}) custom-call(bf16[128,2048]{1,0:T(8,128)(2,1)} %get-tuple-element.6.hid_ref, f32[1,2]{1,0:T(1,128)} %get-tuple-element.7.fv_ref, f32[1,2]{1,0:T(1,128)} %get-tuple-element.8.adv_ref), custom_call_target="tpu_custom_call" | custom-call | tf_op jit(solution)/shard_map/pallas_call | solution.py:820

commit v7 on v6

--- a/solution.py
+++ b/solution.py
@@ -21,8 +21,8 @@
 QSCALE = math.log2(math.e) / math.sqrt(HEAD_DIM)
 NEG = -1e30
 ONWARD = (0, 1)
-HOOKS = (12, 20)
-UNROLL = 4
+HOOKS = (9, 21)
+UNROLL = 3
 
 
 def remote(src, dst, send_sem, recv_sem, where):

time: 109 us -> 107 us (0.982)
  Pallas kernels: 108 us -> 106 us
    pallas_call x1, Pallas kernels: 106 us -> 104 us  [local(): pl.pallas_call(layer_kernel, out_shape=(jax.ShapeDtypeStruct((ROWS, D), B...]
where the time goes in v7:
time: 107 us
  Pallas kernels  106 us (99%)
    pallas_call x1, Pallas kernels, local(): pl.pallas_call(layer_kernel, out_shape=(jax.ShapeDtypeStruct((ROWS, D), B...  104 us

profile of v7, /device:TPU:1, one launch (start us, length us, event | category | flops | bytes accessed | tf_op | source)
XLA Modules:
  0.0 107.1 jit_solution(12023334822197745439)
XLA Ops:
  0.6 104.4 %shard_map.130 = (bf16[128,2048]{1,0:T(8,128)(2,1)}, f32[1,2]{1,0:T(1,128)}, f32[1,2]{1,0:T(1,128)}) custom-call(s32[2]{0:T(128)} %vf_ref.1, bf16[128,2048]{1,0:T(8,128)(2,1)} %bitcast.6, bf16[3,2048,512]{2,1,0:T(8,128)(2,1)} %w_hbm.1, bf16[512,2048]{1,0:T(8,128)(2,1)} %wo_hbm.1, bf16[2048,2048]{1,0:T(8,128)(2,1)} %wu_hbm.1, bf16[2048,2048]{1,0:T(8,128)(2,1)} %wd_hbm.1, ...), custom_call_target="tpu_custom_call" | custom-call | flops 40000000000 | bytes 40000000 | tf_op jit(solution)/shard_map/pallas_call | solution.py:744
  105.0 1.9 %shard_map.131 = (bf16[1,128,2048]{2,1,0:T(8,128)(2,1)}, f32[1,2]{1,0:T(1,128)}, f32[1,2]{1,0:T(1,128)}) custom-call(bf16[128,2048]{1,0:T(8,128)(2,1)} %get-tuple-element.6.hid_ref, f32[1,2]{1,0:T(1,128)} %get-tuple-element.7.fv_ref, f32[1,2]{1,0:T(1,128)} %get-tuple-element.8.adv_ref), custom_call_target="tpu_custom_call" | custom-call | tf_op jit(solution)/shard_map/pallas_call | solution.py:820

commit v8 on v7

--- a/solution.py
+++ b/solution.py
@@ -623,7 +623,7 @@
         for k in (0, 1):
             mine = (z // 2 == k).astype(F32)
             zs[z, k : k + 1, :] = jnp.sum(fs[k] + fs[2] * mine, axis=0, keepdims=True)
-        for d in (1, 2, 3):
+        for d in (2, 1, 3):
             send(zs.at[z], zs.at[z], z_send.at[d - 1], z_recv.at[z], {"tensor": (z + d) % 4})
 
     rs_sums(0)
@@ -633,8 +633,10 @@
         t = (z + d) % 4
         arrive(zs.at[t], z_recv.at[t])
     means[s] = (zs[0] + zs[1] + zs[2] + zs[3]) * (1.0 / TOK_FRAME)
-    for d in range(1, 16):
-        send(means.at[s], means.at[s], s_send.at[d - 1], s_recv.at[s], {"seq": (s + d) % 16})
+    steps = sorted(((dy, dx) for dy in range(4) for dx in range(4)), key=lambda d: -min(d[0], 4 - d[0]) - min(d[1], 4 - d[1]))
+    for k, (dy, dx) in enumerate(steps[:15]):
+        to = {"seq": (s // 4 + dy) % 4 * 4 + (s % 4 + dx) % 4}
+        send(means.at[s], means.at[s], s_send.at[k], s_recv.at[s], to)
     rs_sums(1)
     for d in range(1, 16):
         t = (s + d) % 16

time: 107 us -> 107 us (level)
  no operation moved by 1% of the time
where the time goes in v8:
time: 107 us
  Pallas kernels  106 us (99%)
    pallas_call x1, Pallas kernels, local(): pl.pallas_call(layer_kernel, out_shape=(jax.ShapeDtypeStruct((ROWS, D), B...  104 us

profile of v8, /device:TPU:1, one launch (start us, length us, event | category | flops | bytes accessed | tf_op | source)
XLA Modules:
  0.0 106.8 jit_solution(17957435931797274000)
XLA Ops:
  0.6 104.1 %shard_map.130 = (bf16[128,2048]{1,0:T(8,128)(2,1)}, f32[1,2]{1,0:T(1,128)}, f32[1,2]{1,0:T(1,128)}) custom-call(s32[2]{0:T(128)} %vf_ref.1, bf16[128,2048]{1,0:T(8,128)(2,1)} %bitcast.6, bf16[3,2048,512]{2,1,0:T(8,128)(2,1)} %w_hbm.1, bf16[512,2048]{1,0:T(8,128)(2,1)} %wo_hbm.1, bf16[2048,2048]{1,0:T(8,128)(2,1)} %wu_hbm.1, bf16[2048,2048]{1,0:T(8,128)(2,1)} %wd_hbm.1, ...), custom_call_target="tpu_custom_call" | custom-call | flops 40000000000 | bytes 40000000 | tf_op jit(solution)/shard_map/pallas_call | solution.py:746
  104.8 1.9 %shard_map.131 = (bf16[1,128,2048]{2,1,0:T(8,128)(2,1)}, f32[1,2]{1,0:T(1,128)}, f32[1,2]{1,0:T(1,128)}) custom-call(bf16[128,2048]{1,0:T(8,128)(2,1)} %get-tuple-element.6.hid_ref, f32[1,2]{1,0:T(1,128)} %get-tuple-element.7.fv_ref, f32[1,2]{1,0:T(1,128)} %get-tuple-element.8.adv_ref), custom_call_target="tpu_custom_call" | custom-call | tf_op jit(solution)/shard_map/pallas_call | solution.py:822
